TPU v7x, 256 devices: a whole 4x4x8 slice. The times are simulated.
256 devices in a mesh: member: 2 (over y_hi), seq: 32 (over z, x), head: 4 (over y_lo, core).
Axes of the slice: x: 4, y: 4 (y_hi: 2, y_lo: 2; y = y_hi * 2 + y_lo), z: 8, core: 2. Of those that a mesh axis runs over, the one named last changes fastest.
Arguments:
- tokens: bfloat16 [16384, 5120], P(('seq', 'head')), may hold values from -24 to 24
- lattice: int32 [3, 16384], P(None, 'seq'), may hold values from 0 to 63
- timestep: int32 [32], replicated, may hold values from 0 to 999
- time_weight: bfloat16 [2, 256, 5120], P(None, None, 'seq'), may hold values from -0.375 to 0.375
- query_weight: bfloat16 [2, 5120, 2560], P('member', 'seq', 'head'), may hold values from -6 to 6
- key_weight: bfloat16 [5120, 2560], P('seq', 'head'), may hold values from -6 to 6
- values: bfloat16 [16384, 2560], P(('seq', 'head')), may hold values from -6 to 6
- cotangent: bfloat16 [2, 16384, 2560], P('member', ('seq', 'head')), may hold values from -72 to 72
Outputs:
- fisher: float32 [2, 5120, 2560], P('member', 'seq', 'head')
- merged: float32 [5120, 2560], P('seq', 'head')
All inputs are finite; a program needn't handle non-finite values.
Results may differ from a plain program's by a relative error of at most 0.022.
Values may be sent and summed in bfloat16 or wider, within the bound.
A program may use at most 128 MiB of HBM per device.

v0:
```python
import math

import jax
import jax.numpy as jnp
from jax import lax
from jax.sharding import Mesh
from jax.sharding import PartitionSpec as P

HEAD_SIZE = 128
SEQ = ("seq_0", "seq_1")
SEQ_HEAD = ("seq_0", "seq_1", "head")


damping = 0.01


def side_by_side(arrays, axis, dim, along):
    widths = [a.shape[along] for a in arrays]
    both = jnp.concatenate(arrays, axis=along)
    out = lax.all_gather(both, axis, axis=dim, tiled=True)
    return tuple(jnp.split(out, [sum(widths[:k]) for k in range(1, len(widths))], axis=along))


def own_rows(terms, axes):
    subtotal = terms.astype(jnp.bfloat16)
    for axis in axes:
        subtotal = lax.psum_scatter(subtotal, axis, scatter_dimension=0, tiled=True)
    return subtotal.astype(jnp.float32)


def copy_for_each(array, axis):
    size = lax.axis_size(axis)
    return lax.all_to_all(
        jnp.broadcast_to(array[None], (size, *array.shape)), axis, 0, 0, tiled=True
    )


def of_everyone(array, axis):
    everything = copy_for_each(array, axis)
    return jnp.sum(everything.astype(jnp.float32), axis=0)


def time_features(timestep, feature_count):
    halfway = feature_count // 2
    ladder = jnp.arange(halfway).astype(jnp.float32)
    frequency = jnp.exp(-math.log(10000.0) * 2.0 * ladder / feature_count)
    angles = timestep.astype(jnp.float32)[:, None] * frequency[None, :]
    return jnp.concatenate([jnp.cos(angles), jnp.sin(angles)], axis=1).astype(jnp.bfloat16)


def rope_tables(lattice, head_width):
    halfway = head_width // 2
    side_pairs = head_width // 6
    frame_pairs = halfway - 2 * side_pairs
    column = jnp.arange(head_width)
    pair_index = column % halfway
    which_axis = jnp.where(
        pair_index < frame_pairs, 0, jnp.where(pair_index < frame_pairs + side_pairs, 1, 2)
    )
    anchor = jnp.where(
        which_axis == 0, 0, jnp.where(which_axis == 1, frame_pairs, frame_pairs + side_pairs)
    )
    pair_span = jnp.where(which_axis == 0, frame_pairs, side_pairs)
    frequency = jnp.exp(
        -math.log(10000.0)
        * (pair_index - anchor).astype(jnp.float32)
        / pair_span.astype(jnp.float32)
    )
    position = lattice.astype(jnp.float32)
    angles = jnp.zeros((lattice.shape[1], head_width), jnp.float32)
    for axis_number in range(3):
        chosen = jnp.where(which_axis == axis_number, frequency, 0.0)
        angles = angles + position[axis_number][:, None] * chosen[None, :]
    sign_flip = jnp.where(column < halfway, -1.0, 1.0).astype(jnp.float32)
    return (jnp.cos(angles), jnp.sin(angles) * sign_flip[None, :])


def normed_rotation(stacked, cosine, sine_table):
    halfway = stacked.shape[2] // 2
    inverse = lax.rsqrt(jnp.mean(stacked * stacked, axis=2, keepdims=True) + 1e-06)
    normed = stacked * inverse
    rotated = (
        normed * cosine[:, None, :] + jnp.roll(normed, halfway, axis=2) * sine_table[:, None, :]
    )
    return (normed, inverse, rotated)


def attention_backward(query_pre, key_pre, values, cotangent, cosine, sine_table, head_width):
    length, width = query_pre.shape
    head_count = width // head_width
    halfway = head_width // 2
    query_normed, query_inverse, query_rotated = normed_rotation(
        query_pre.reshape(length, head_count, head_width), cosine, sine_table
    )
    unused_normed, unused_inverse, key_rotated = normed_rotation(
        key_pre.reshape(length, head_count, head_width), cosine, sine_table
    )
    query_round = query_rotated.astype(jnp.bfloat16)
    key_round = key_rotated.astype(jnp.bfloat16)
    value_heads = values.reshape(length, head_count, head_width)
    block_rows = min(length, 512)
    block_count = length // block_rows
    score_scale = head_width ** (-0.5)

    def one_block(portion):
        query_block, grad_block = portion
        scores = (
            jnp.einsum("qhd,khd->hqk", query_block, key_round, preferred_element_type=jnp.float32)
            * score_scale
        )
        raised = jnp.exp(scores)
        weights = raised / jnp.sum(raised, axis=2, keepdims=True)
        rounded = weights.astype(jnp.bfloat16)
        attended = jnp.einsum(
            "hqk,khd->qhd", rounded, value_heads, preferred_element_type=jnp.float32
        )
        inner = jnp.sum(grad_block.astype(jnp.float32) * attended, axis=2)
        grad_weights = jnp.einsum(
            "qhd,khd->hqk", grad_block, value_heads, preferred_element_type=jnp.float32
        )
        grad_scores = (weights * (grad_weights - inner.T[:, :, None])).astype(jnp.bfloat16)
        return (
            jnp.einsum("hqk,khd->qhd", grad_scores, key_round, preferred_element_type=jnp.float32)
            * score_scale
        )

    grad_rotated = lax.map(
        one_block,
        (
            query_round.reshape(block_count, block_rows, head_count, head_width),
            cotangent.reshape(block_count, block_rows, head_count, head_width),
        ),
    )
    grad_rotated = grad_rotated.reshape(length, head_count, head_width)
    grad_normed = grad_rotated * cosine[:, None, :] + jnp.roll(
        grad_rotated * sine_table[:, None, :], halfway, axis=2
    )
    grad_query = query_inverse * (
        grad_normed - query_normed * jnp.mean(grad_normed * query_normed, axis=2, keepdims=True)
    )
    return grad_query.reshape(length, width).astype(jnp.bfloat16)


def on_device(tokens, lattice, timestep, time_weight, query_weight, key_weight, values, cotangent):
    features = time_features(timestep, time_weight.shape[1])
    local_shift = jnp.einsum(
        "cf,jfd->cjd", features, time_weight, preferred_element_type=jnp.float32
    )
    own_shift = lax.all_to_all(
        local_shift.astype(jnp.bfloat16), SEQ, split_axis=0, concat_axis=2, tiled=True
    ).astype(local_shift.dtype)
    hidden = tokens.astype(jnp.float32)
    average = jnp.mean(hidden, axis=1, keepdims=True)
    centred = hidden - average
    variance = jnp.mean(centred * centred, axis=1, keepdims=True)
    normed = centred * lax.rsqrt(variance + 1e-06)
    modulated = (normed * (1.0 + own_shift[0, 1][None, :]) + own_shift[0, 0][None, :]).astype(
        jnp.bfloat16
    )
    clip_rows = lax.all_gather(modulated, "head", axis=0, tiled=True)
    cosine, sine_table = rope_tables(lattice, HEAD_SIZE)
    own_query = query_weight[0]

    def contract(portion):
        return jnp.dot(clip_rows, portion, preferred_element_type=jnp.float32)

    portions = side_by_side((own_query, key_weight), SEQ, 0, 1)
    query_pre = contract(portions[0])
    key_pre = contract(portions[1])
    value_heads, cot_heads = (
        lax.all_to_all(values, "head", split_axis=1, concat_axis=0, tiled=True),
        lax.all_to_all(cotangent[0], "head", split_axis=1, concat_axis=0, tiled=True),
    )
    grad_query = attention_backward(
        query_pre, key_pre, value_heads, cot_heads, cosine, sine_table, HEAD_SIZE
    )
    grad = lax.dot_general(
        clip_rows, grad_query, (((0,), (0,)), ((), ())), preferred_element_type=jnp.float32
    )
    fisher = own_rows(grad * grad, SEQ)
    weighted = fisher + damping
    upper = weighted * own_query.astype(jnp.float32)
    upper_sum, lower_sum = (
        of_everyone(upper.astype(jnp.bfloat16), "member").astype(jnp.float32),
        of_everyone(weighted.astype(jnp.bfloat16), "member").astype(jnp.float32),
    )
    merged = upper_sum / lower_sum
    return (fisher[None], merged)


def solution(mesh):
    finer = Mesh(
        mesh.devices.reshape(mesh.shape["member"], 8, 4, mesh.shape["head"]),
        ("member", "seq_0", "seq_1", "head"),
    )
    in_specs = (
        P(SEQ_HEAD, None),
        P(None, SEQ),
        P(),
        P(None, None, SEQ),
        P("member", SEQ, "head"),
        P(SEQ, "head"),
        P(SEQ_HEAD, None),
        P("member", SEQ_HEAD, None),
    )
    out_specs = (P("member", SEQ, "head"), P(SEQ, "head"))
    return jax.shard_map(
        on_device, mesh=finer, in_specs=in_specs, out_specs=out_specs, check_vma=False
    )
```

profile of v0, /device:TPU:1, one launch (start us, length us, event | category | flops | bytes accessed | tf_op | source)
XLA Modules:
  0.0 384.5 jit_solution(6202035833007734098)
XLA Ops:
  7.2 0.8 convert_element_type.123
  8.1 0.1 convolution_convert_fusion
  8.3 0.7 copy.51
  8.9 11.9 %all-to-all-start = ((bf16[32,2,160]{2,1,0:T(2,128)(2,1)}), bf16[32,2,160]{2,1,0:T(2,128)(2,1)S(1)}, u32[]{:S(2)}, u32[]{:S(2)}) async-start(bf16[32,2,160]{2,1,0:T(2,128)(2,1)} %copy.51), calls=%async_computation | async-start | bytes 65536 | tf_op jit(solution)/shard_map/all_to_all | solution.py:149
  20.9 1.6 convert_reduce_fusion
  22.5 0.5 fusion.8
  23.0 6.5 %all-to-all-done = bf16[32,2,160]{2,1,0:T(2,128)(2,1)S(1)} async-done(((bf16[32,2,160]{2,1,0:T(2,128)(2,1)}), bf16[32,2,160]{2,1,0:T(2,128)(2,1)S(1)}, u32[]{:S(2)}, u32[]{:S(2)}) %all-to-all-start) | async-done | bytes 20512 | tf_op jit(solution)/shard_map/all_to_all | solution.py:149
  29.7 1.7 fusion.11
  31.4 0.9 copy-done.6
  32.4 0.8 pad_maximum_fusion
  33.2 1.1 copy.59
  34.3 5.6 %all-to-all-start.2 = ((bf16[128,4,640]{0,2,1:T(8,128)(2,1)}), bf16[128,4,640]{0,2,1:T(8,128)(2,1)S(1)}, u32[]{:S(2)}, u32[]{:S(2)}) async-start(bf16[128,4,640]{0,2,1:T(8,128)(2,1)} %bitcast.13), calls=%async_computation.2 | async-start | bytes 1310720 | tf_op jit(solution)/shard_map/all_to_all | solution.py:171
  39.9 1.1 copy.57
  41.0 13.3 %all-to-all-done.2 = bf16[128,4,640]{0,2,1:T(8,128)(2,1)S(1)} async-done(((bf16[128,4,640]{0,2,1:T(8,128)(2,1)}), bf16[128,4,640]{0,2,1:T(8,128)(2,1)S(1)}, u32[]{:S(2)}, u32[]{:S(2)}) %all-to-all-start.2) | async-done | bytes 655392 | tf_op jit(solution)/shard_map/all_to_all | solution.py:171
  54.2 5.5 %all-to-all-start.1 = ((bf16[128,4,640]{0,2,1:T(8,128)(2,1)}), bf16[128,4,640]{0,2,1:T(8,128)(2,1)S(1)}, u32[]{:S(2)}, u32[]{:S(2)}) async-start(bf16[128,4,640]{0,2,1:T(8,128)(2,1)} %bitcast.11), calls=%async_computation.1 | async-start | bytes 1310720 | tf_op jit(solution)/shard_map/all_to_all | solution.py:172
  59.7 2.0 broadcast_multiply_fusion.3
  61.8 0.5 copy.60
  62.3 1.1 reshape.305
  63.4 13.3 %all-to-all-done.1 = bf16[128,4,640]{0,2,1:T(8,128)(2,1)S(1)} async-done(((bf16[128,4,640]{0,2,1:T(8,128)(2,1)}), bf16[128,4,640]{0,2,1:T(8,128)(2,1)S(1)}, u32[]{:S(2)}, u32[]{:S(2)}) %all-to-all-start.1) | async-done | bytes 655392 | tf_op jit(solution)/shard_map/all_to_all | solution.py:172
  76.6 0.5 copy.58
  77.1 1.1 squeeze.12
  78.2 20.7 %all-gather.3.cloned.1.call-done = bf16[512,5120]{1,0:T(8,128)(2,1)} async-done(((bf16[128,5120]{1,0:T(8,128)(2,1)}), bf16[512,5120]{1,0:T(8,128)(2,1)}) %all-gather.3.cloned.1.call-update) | async-done | bytes 5242896 | tf_op jit(solution)/shard_map/all_gather | solution.py:160
  98.9 118.5 %all-gather.5.cloned.1.call-done = bf16[5120,1280]{1,0:T(8,128)(2,1)} async-done(((bf16[160,1280]{1,0:T(8,128)(2,1)}), bf16[5120,1280]{1,0:T(8,128)(2,1)}) %all-gather.5.cloned.1.call-update) | async-done | bytes 13107216 | tf_op jit(solution)/shard_map/all_gather | solution.py:20
  217.4 8.4 %fusion = f32[512,640]{0,1:T(8,128)S(1)} fusion(bf16[512,5120]{1,0:T(8,128)(2,1)} %all-gather.3.cloned.1.call-done, bf16[5120,1280]{1,0:T(8,128)(2,1)} %all-gather.5.cloned.1.call-done), kind=kOutput, calls=%fused_computation.1 | convolution fusion | flops 3355443200 | bytes 13107200 | tf_op jit(solution)/shard_map/dot_general | solution.py:165
  225.8 0.2 multiply_reduce_fusion.1
  226.2 2.2 copy-done.15
  228.5 6.0 %fusion.2 = f32[512,640]{0,1:T(8,128)S(1)} fusion(bf16[512,5120]{1,0:T(8,128)(2,1)S(1)} %copy-done.15, bf16[5120,1280]{1,0:T(8,128)(2,1)} %all-gather.5.cloned.1.call-done), kind=kOutput, calls=%fused_computation.3 | convolution fusion | flops 3355443200 | bytes 13107200 | tf_op jit(solution)/shard_map/dot_general | solution.py:165
  234.5 0.2 multiply_reduce_fusion.2
  234.9 0.8 copy-done.4
  235.8 0.4 fusion.28
  236.2 1.2 fusion.5
  237.5 1.2 fusion.31
  238.7 1.1 copy-done.2
  239.8 5.9 %broadcast_multiply_fusion = (f32[512,5,128]{0,2,1:T(8,128)}, f32[512,5,128]{0,2,1:T(8,128)S(1)}) fusion(f32[512,128]{0,1:T(8,128)} %get-tuple-element.30, bf16[512,5,128]{0,2,1:T(8,128)(2,1)S(1)} %fusion.28, bf16[512,5,128]{0,2,1:T(8,128)(2,1)} %squeeze.12, bf16[512,5,128]{0,2,1:T(8,128)(2,1)} %reshape.305, f32[5,512]{1,0:T(8,128)S(1)} %bitcast.67, ...), kind=kOutput, calls=%fused_computation.41 | convolution fusion | flops 677969920 | bytes 10113024 | tf_op jit(solution)/shard_map/while/body/eval_jaxpr/hqk,khd->qhd/dot_general | solution.py:123
  245.7 1.6 fusion.53
  247.3 0.5 multiply_reduce_fusion
  247.8 0.6 multiply_convert_fusion.5
  248.4 0.4 slice-done.1
  248.9 6.3 %multiply_convert_fusion = bf16[5120,640]{1,0:T(8,128)(2,1)} fusion(bf16[512,5120]{1,0:T(8,128)(2,1)S(1)} %bitcast.66, bf16[512,640]{0,1:T(8,128)(2,1)S(1)} %bitcast.59), kind=kOutput, calls=%fused_computation | convolution fusion | flops 3361996800 | bytes 12451840 | tf_op jit(solution)/shard_map/dot_general | solution.py:177
  255.2 75.5 %reduce-scatter.3.cloned.1.call-done = bf16[640,640]{1,0:T(8,128)(2,1)} async-done(((bf16[5120,640]{1,0:T(8,128)(2,1)}), bf16[640,640]{1,0:T(8,128)(2,1)}) %reduce-scatter.3.cloned.1.call-update) | async-done | bytes 819216 | tf_op jit(solution)/shard_map/reduce_scatter | solution.py:27
  330.7 25.0 %reduce-scatter.5.cloned.1.call-done = bf16[160,640]{1,0:T(8,128)(2,1)} async-done(((bf16[640,640]{1,0:T(8,128)(2,1)}), bf16[160,640]{1,0:T(8,128)(2,1)}) %reduce-scatter.5.cloned.1.call-update) | async-done | bytes 204816 | tf_op jit(solution)/shard_map/reduce_scatter | solution.py:27
  355.7 1.0 fusion.38
  356.8 9.7 %all_to_all.51 = bf16[2,160,640]{2,1,0:T(8,128)(2,1)S(1)} all-to-all(bf16[2,160,640]{2,1,0:T(8,128)(2,1)S(1)} %broadcast_in_dim.82), channel_id=1, replica_groups=mesh['member'=2,'seq_0'=8,'seq_1'=4,'head'=4] {'member'}, dimensions={0} | all-to-all | bytes 819200 | tf_op jit(solution)/shard_map/all_to_all | solution.py:33
  366.5 0.8 broadcast_in_dim.81
  367.2 3.5 all-to-all-start.3
  370.7 0.8 convert_bitcast_fusion
  371.6 5.5 %all-to-all-done.3 = bf16[2,160,640]{2,1,0:T(8,128)(2,1)S(1)} async-done(((bf16[2,160,640]{2,1,0:T(8,128)(2,1)}), bf16[2,160,640]{2,1,0:T(8,128)(2,1)S(1)}, u32[]{:S(2)}, u32[]{:S(2)}) %all-to-all-start.3) | async-done | bytes 409632 | tf_op jit(solution)/shard_map/all_to_all | solution.py:33
  377.1 0.9 div.63
  (62 shorter events, 1.5 us)
Async XLA Ops:
  7.2 1.0 copy-start
  7.2 15.3 %copy-start.1 = (bf16[128,5120]{1,0:T(8,128)(2,1)S(1)}, bf16[128,5120]{1,0:T(8,128)(2,1)}, u32[]{:S(2)}) copy-start(bf16[128,5120]{1,0:T(8,128)(2,1)} %param.8) | copy-start | bytes 3932164
  8.9 20.6 %all-to-all-start = ((bf16[32,2,160]{2,1,0:T(2,128)(2,1)}), bf16[32,2,160]{2,1,0:T(2,128)(2,1)S(1)}, u32[]{:S(2)}, u32[]{:S(2)}) async-start(bf16[32,2,160]{2,1,0:T(2,128)(2,1)} %copy.51), calls=%async_computation | async-start | bytes 65536 | tf_op jit(solution)/shard_map/all_to_all | solution.py:149
  20.8 78.1 %all-gather.3.cloned.1.call-start = ((), (), s32[]{:S(2)}) async-start(), calls=%async_computation.7 | async-start | bytes 6553600 | tf_op jit(solution)/shard_map/all_gather | solution.py:160
  31.4 0.9 copy-start.6
  31.4 1.0 copy-start.13
  31.4 1.8 copy-start.9
  31.4 186.0 %all-gather.5.cloned.1.call-start = ((), (), s32[]{:S(2)}) async-start(), calls=%async_computation.8 | async-start | bytes 13516800 | tf_op jit(solution)/shard_map/all_gather | solution.py:20
  33.2 6.7 %copy-start.10 = (bf16[1,128,2560]{2,1,0:T(8,128)(2,1)S(1)}, bf16[1,128,2560]{2,1,0:T(8,128)(2,1)}, u32[]{:S(2)}) copy-start(bf16[1,128,2560]{2,1,0:T(8,128)(2,1)} %param.15) | copy-start | bytes 1966084
  34.3 19.9 %all-to-all-start.2 = ((bf16[128,4,640]{0,2,1:T(8,128)(2,1)}), bf16[128,4,640]{0,2,1:T(8,128)(2,1)S(1)}, u32[]{:S(2)}, u32[]{:S(2)}) async-start(bf16[128,4,640]{0,2,1:T(8,128)(2,1)} %bitcast.13), calls=%async_computation.2 | async-start | bytes 1310720 | tf_op jit(solution)/shard_map/all_to_all | solution.py:171
  39.9 19.8 %copy-start.14 = (s32[3,512]{1,0:T(4,128)S(1)}, s32[3,512]{1,0:T(4,128)}, u32[]{:S(2)}) copy-start(s32[3,512]{1,0:T(4,128)} %param.9) | copy-start | bytes 18436
  54.2 22.4 %all-to-all-start.1 = ((bf16[128,4,640]{0,2,1:T(8,128)(2,1)}), bf16[128,4,640]{0,2,1:T(8,128)(2,1)S(1)}, u32[]{:S(2)}, u32[]{:S(2)}) async-start(bf16[128,4,640]{0,2,1:T(8,128)(2,1)} %bitcast.11), calls=%async_computation.1 | async-start | bytes 1310720 | tf_op jit(solution)/shard_map/all_to_all | solution.py:172
  59.7 271.0 %reduce-scatter.3.cloned.1.call-start = ((), (), s32[]{:S(2)}) async-start(), calls=%async_computation.9 | async-start | bytes 7372800 | tf_op jit(solution)/shard_map/reduce_scatter | solution.py:27
  226.0 2.5 copy-start.15
  234.8 1.0 copy-start.4
  234.8 1.0 copy-start.5
  236.2 1.3 copy-start.11
  236.2 1.3 copy-start.12
  237.5 2.3 copy-start.2
  245.7 1.6 copy-start.3
  245.7 2.7 slice-start
  247.3 1.6 slice-start.1
  255.1 100.6 %copy-start.7 = (bf16[1,160,640]{2,1,0:T(8,128)(2,1)S(1)}, bf16[1,160,640]{2,1,0:T(8,128)(2,1)}, u32[]{:S(2)}) copy-start(bf16[1,160,640]{2,1,0:T(8,128)(2,1)} %param.12) | copy-start | bytes 614404
  255.1 100.6 %reduce-scatter.5.cloned.1.call-start = ((), (), s32[]{:S(2)}) async-start(), calls=%async_computation.10 | async-start | bytes 1024000 | tf_op jit(solution)/shard_map/reduce_scatter | solution.py:27
  356.7 14.0 %copy-start.8 = (bf16[160,640]{1,0:T(8,128)(2,1)S(1)}, bf16[160,640]{1,0:T(8,128)(2,1)}, u32[]{:S(2)}) copy-start(bf16[160,640]{1,0:T(8,128)(2,1)} %reduce-scatter.5.cloned.1.call-done) | copy-start | bytes 614404
  367.2 9.8 %all-to-all-start.3 = ((bf16[2,160,640]{2,1,0:T(8,128)(2,1)}), bf16[2,160,640]{2,1,0:T(8,128)(2,1)S(1)}, u32[]{:S(2)}, u32[]{:S(2)}) async-start(bf16[2,160,640]{2,1,0:T(8,128)(2,1)} %broadcast_in_dim.81), calls=%async_computation.5 | async-start | bytes 819200 | tf_op jit(solution)/shard_map/all_to_all | solution.py:33
Sparse Core Ops, SparseCore 0:
  31.5 67.3 all-gather.2
  102.1 115.2 all-gather.4
  255.3 75.3 reduce-scatter.2
  333.1 22.5 reduce-scatter.4
where the time goes:
time: 388 us; the launch traced here: 384 us
  waiting for transfers between devices  278 us (72%)
  matrix products  29.1 us (8%)
  starting transfers between devices  26.5 us (7%)
  local copies, waits for them, and re-layouts  14.4 us (4%)
  between operations  14.1 us (4%)
  other arithmetic  12.4 us (3%)
  blocking collectives  9.69 us (2%)
    all_gather x1, waiting for transfers between devices, side_by_side(): out = lax.all_gather(both, axis, axis=dim, tiled=True)  118 us
    reduce_scatter x2, waiting for transfers between devices, own_rows(): subtotal = lax.psum_scatter(subtotal, axis, scatter_dimension=0, tiled=True)  100 us
    all_gather x1, waiting for transfers between devices, on_device(): clip_rows = lax.all_gather(modulated, 'head', axis=0, tiled=True)  20.7 us
    dot_general x2, matrix products, contract(): return jnp.dot(clip_rows, portion, preferred_element_type=jnp.float32)  14.4 us
    all_to_all x1, waiting for transfers between devices, on_device(): lax.all_to_all(values, 'head', split_axis=1, concat_axis=0, tiled=True)  13.3 us
    all_to_all x1, waiting for transfers between devices, on_device(): lax.all_to_all(cotangent[0], 'head', split_axis=1, concat_axis=0, tiled=T...  13.3 us
    all_to_all x1, starting transfers between devices, on_device(): lax.all_to_all(local_shift.astype(jnp.bfloat16), SEQ, split_axis=0, conca...  11.9 us
    all_to_all x1, blocking collectives, copy_for_each(): lax.all_to_all(jnp.broadcast_to(array[None], (size, *array.shape)), axis,...  9.69 us
  transfers between devices with their start and end apart: 8, of which 8 were waited for; matrix products, arithmetic and copies ran while one was open for 3% of the time, Pallas kernels for 0%

commit v1 on v0

v1 whole, which is shorter than its diff:
```python
import functools
import math

import jax
import jax.numpy as jnp
from jax import lax
from jax.experimental import pallas as pl
from jax.experimental.pallas import tpu as pltpu
from jax.sharding import Mesh
from jax.sharding import PartitionSpec as P

HEAD_SIZE = 128
AXES = ("member", "z", "x", "ylo", "core")
SEQ = ("z", "x")
HEAD = ("ylo", "core")
SEQ_HEAD = ("z", "x", "ylo", "core")
MESH = pl.DeviceIdType.MESH

damping = 0.01
SLICE = 160
HALF = 320
KHEADS = 3
ROW_CHUNK = 32


def time_features(timestep, feature_count):
    halfway = feature_count // 2
    ladder = jnp.arange(halfway).astype(jnp.float32)
    frequency = jnp.exp(-math.log(10000.0) * 2.0 * ladder / feature_count)
    angles = timestep.astype(jnp.float32)[:, None] * frequency[None, :]
    return jnp.concatenate([jnp.cos(angles), jnp.sin(angles)], axis=1).astype(jnp.bfloat16)


def rope_tables(lattice, head_width):
    halfway = head_width // 2
    side_pairs = head_width // 6
    frame_pairs = halfway - 2 * side_pairs
    column = jnp.arange(head_width)
    pair_index = column % halfway
    which_axis = jnp.where(
        pair_index < frame_pairs, 0, jnp.where(pair_index < frame_pairs + side_pairs, 1, 2)
    )
    anchor = jnp.where(
        which_axis == 0, 0, jnp.where(which_axis == 1, frame_pairs, frame_pairs + side_pairs)
    )
    pair_span = jnp.where(which_axis == 0, frame_pairs, side_pairs)
    frequency = jnp.exp(
        -math.log(10000.0)
        * (pair_index - anchor).astype(jnp.float32)
        / pair_span.astype(jnp.float32)
    )
    position = lattice.astype(jnp.float32)
    angles = jnp.zeros((lattice.shape[1], head_width), jnp.float32)
    for axis_number in range(3):
        chosen = jnp.where(which_axis == axis_number, frequency, 0.0)
        angles = angles + position[axis_number][:, None] * chosen[None, :]
    sign_flip = jnp.where(column < halfway, -1.0, 1.0).astype(jnp.float32)
    return (jnp.cos(angles), jnp.sin(angles) * sign_flip[None, :])


def place():
    return tuple(lax.axis_index(a) for a in AXES)


def remote(src, dst, send, recv, to):
    return pltpu.make_async_remote_copy(
        src_ref=src, dst_ref=dst, send_sem=send, recv_sem=recv, device_id=to, device_id_type=MESH
    )


def hello(to):
    pl.semaphore_signal(pltpu.get_barrier_semaphore(), inc=1, device_id=to, device_id_type=MESH)


def gather_kernel(
    tok, shl, w, val, cot, rows, big, vals, cots,
    made, buf1, tot, buf2, mod,
    s_m1, r_m1, s_m2, r_m2, s_s1, r_s1, s_rg, r_rg, s_dd, r_dd,
    s_r1, r_r1, s_r2, r_r2, s_v, r_v,
):
    m, z, x, yl, c = place()
    px, pair, hh = lax.rem(x, 2), x // 2, x // 2
    sib = (m, z, x, yl, 1 - c)
    dz = 1 - 2 * c
    znext = lax.rem(z + dz + 8, 8)
    xc = 2 * pair + c
    home = c == px
    up = (jnp.where(yl == 0, m, 1 - m), z, x, 1 - yl, c)
    down = (jnp.where(yl == 0, 1 - m, m), z, x, 1 - yl, c)

    for j in range(1, 16):
        q = lax.rem(x * 4 + yl * 2 + c + j, 16)
        hello((m, z, q // 4, lax.rem(q, 4) // 2, lax.rem(q, 2)))
    for j in range(1, 8):
        hello((m, lax.rem(z + j, 8), x, yl, c))
    hello((1 - m, z, x, 1 - yl, c))
    pl.semaphore_wait(pltpu.get_barrier_semaphore(), 23)

    def m1(j):
        to = lax.rem(x + j, 4)
        return remote(shl.at[to], buf1.at[x], s_m1.at[j], r_m1.at[j], (m, z, to, yl, c))

    for j in range(1, 4):
        m1(j).start()

    def s1(t):
        return remote(
            w, big.at[z, pl.ds(x * SLICE, SLICE), :], s_s1.at[t], r_s1.at[lax.rem(x, 2)],
            (m, z, c + 2 * t, yl, hh),
        )

    for t in range(2):
        own = (c + 2 * t == x) & (hh == c)

        @pl.when(jnp.logical_not(own))
        def _():
            s1(t).start()

        @pl.when(own)
        def _():
            big[z, pl.ds(pl.multiple_of(x * SLICE, SLICE), SLICE), :] = w[...]

    buf1[x] = shl[x]
    for j in range(1, 4):
        m1(j).wait_recv()
    tot[...] = buf1[0] + buf1[1] + buf1[2] + buf1[3]

    def m2(j):
        to = lax.rem(z + j, 8)
        return remote(tot.at[to], buf2.at[z], s_m2.at[j], r_m2.at[j], (m, to, x, yl, c))

    for j in range(1, 8):
        m2(j).start()
    buf2[z] = tot[z]

    def half_of(n):
        return c if n % 2 == 0 else 1 - c

    def ring(n):
        origin = lax.rem(z - dz * (n // 2) + 8, 8)
        spot = big.at[origin, pl.ds(half_of(n) * HALF, HALF), :]
        return remote(spot, spot, s_rg.at[n], r_rg.at[n], (m, znext, x, yl, c))

    def across(n):
        k = n - 1
        if n == 0:
            spot = big.at[z, pl.ds(c * HALF, HALF), :]
        else:
            origin = lax.rem(z - dz * (k // 2 + 1) + 8, 8)
            spot = big.at[origin, pl.ds(half_of(k) * HALF, HALF), :]
        return remote(spot, spot, s_dd.at[n], r_dd.at[n], sib)

    for u in range(2):
        own = (2 * c + u == x) & home

        @pl.when(jnp.logical_not(own))
        def _():
            remote(
                w, big.at[z, pl.ds((2 * c + u) * SLICE, SLICE), :], s_s1.at[0], r_s1.at[u], sib
            ).wait_recv()

    ring(0).start()
    across(0).start()

    for j in range(1, 8):
        m2(j).wait_recv()
    for k in range(8):
        mod[:, k * 640 : (k + 1) * 640] = buf2[k]

    def r1(t, k):
        return remote(
            made.at[pl.ds(k * ROW_CHUNK, ROW_CHUNK), :],
            rows.at[pl.ds((2 * yl + c) * 128 + k * ROW_CHUNK, ROW_CHUNK), :],
            s_r1.at[t, k], r_r1.at[c, k], (m, z, 2 * pair + t, yl, px),
        )

    for k in range(4):

        @pl.loop(0, ROW_CHUNK // 16)
        def _(i):
            at = pl.multiple_of(k * ROW_CHUNK + i * 16, 16)
            hidden = tok[pl.ds(at, 16), :].astype(jnp.float32)
            average = jnp.mean(hidden, axis=1, keepdims=True)
            centred = hidden - average
            variance = jnp.mean(centred * centred, axis=1, keepdims=True)
            normed = centred * lax.rsqrt(variance + 1e-06)
            out = normed * (1.0 + mod[1:2, :]) + mod[0:1, :]
            made[pl.ds(at, 16), :] = out.astype(jnp.bfloat16)

        for t in range(2):
            own = (2 * pair + t == x) & home

            @pl.when(jnp.logical_not(own))
            def _():
                r1(t, k).start()

            @pl.when(own)
            def _():
                at = pl.multiple_of((2 * yl + c) * 128 + k * ROW_CHUNK, ROW_CHUNK)
                rows[pl.ds(at, ROW_CHUNK), :] = made[k * ROW_CHUNK : (k + 1) * ROW_CHUNK, :]

    across(0).wait_recv()
    ring(1).start()

    def share(a, t, y2):
        h2 = 2 * y2 + t
        src, dst = (val, vals) if a == 0 else (cot, cots)
        return remote(
            src.at[:, h2 * 640 : (h2 + 1) * 640],
            dst.at[pl.ds((2 * yl + c) * 128, 128), :],
            s_v.at[a, t, y2], r_v.at[a, 2 * yl + c], (m, z, 2 * pair + t, y2, px),
        )

    for t in range(2):
        for y2 in range(2):
            own = (2 * pair + t == x) & (y2 == yl) & home

            @pl.when(jnp.logical_not(own))
            def _():
                share(0, t, y2).start()
                share(1, t, y2).start()

            @pl.when(own)
            def _():
                h2 = 2 * y2 + t
                at = pl.multiple_of((2 * yl + c) * 128, 128)
                vals[pl.ds(at, 128), :] = val[:, h2 * 640 : (h2 + 1) * 640]
                cots[pl.ds(at, 128), :] = cot[:, h2 * 640 : (h2 + 1) * 640]

    def r2(p, k, ylo):
        spot = rows.at[pl.ds((2 * ylo + p) * 128 + k * ROW_CHUNK, ROW_CHUNK), :]
        return remote(spot, spot, s_r2.at[p, k], r_r2.at[p, k], up if p == 0 else down)

    for k in range(7):
        if k < 4:
            for p in range(2):
                own = home & (c == p)

                @pl.when(jnp.logical_not(own))
                def _():
                    spot = rows.at[pl.ds((2 * yl + p) * 128 + k * ROW_CHUNK, ROW_CHUNK), :]
                    remote(
                        made.at[pl.ds(k * ROW_CHUNK, ROW_CHUNK), :],
                        spot, s_r1.at[0, k], r_r1.at[p, k], sib,
                    ).wait_recv()

                r2(p, k, yl).start()
        ring(k).wait_recv()
        if k + 2 < 7:
            ring(k + 2).start()
        across(k + 1).start()

    for k in range(4):
        for p in range(2):
            r2(p, k, 1 - yl).wait_recv()
    for hd in range(4):
        own = home & (hd == 2 * yl + c)

        @pl.when(jnp.logical_not(own))
        def _():
            for a, (src, dst) in enumerate(((val, vals), (cot, cots))):
                remote(
                    src.at[:, 0:640], dst.at[hd * 128 : (hd + 1) * 128, :],
                    s_v.at[a, 0, 0], r_v.at[a, hd], sib,
                ).wait_recv()

    for n in range(1, 8):
        across(n).wait_recv()

    for j in range(1, 4):
        m1(j).wait_send()
    for j in range(1, 8):
        m2(j).wait_send()
    for t in range(2):
        own = (c + 2 * t == x) & (hh == c)

        @pl.when(jnp.logical_not(own))
        def _():
            s1(t).wait_send()

        own_r = (2 * pair + t == x) & home

        @pl.when(jnp.logical_not(own_r))
        def _():
            for k in range(4):
                r1(t, k).wait_send()

        for y2 in range(2):
            own_v = (2 * pair + t == x) & (y2 == yl) & home

            @pl.when(jnp.logical_not(own_v))
            def _():
                share(0, t, y2).wait_send()
                share(1, t, y2).wait_send()

    for n in range(7):
        ring(n).wait_send()
    for n in range(8):
        across(n).wait_send()
    for k in range(4):
        for p in range(2):
            r2(p, k, yl).wait_send()


def gather(tok, shl, w, val, cot):
    bf, f32 = jnp.bfloat16, jnp.float32
    width = w.shape[1]
    vmem = pl.BlockSpec(memory_space=pltpu.VMEM)
    dma = pltpu.SemaphoreType.DMA
    return pl.pallas_call(
        gather_kernel,
        out_shape=(
            jax.ShapeDtypeStruct((512, 5120), bf),
            jax.ShapeDtypeStruct((8, 640, width), bf),
            jax.ShapeDtypeStruct((512, 640), bf),
            jax.ShapeDtypeStruct((512, 640), bf),
        ),
        in_specs=[vmem] * 5,
        out_specs=(vmem,) * 4,
        scratch_shapes=[
            pltpu.VMEM((128, 5120), bf),
            pltpu.VMEM((4, 8, 2, 640), f32),
            pltpu.VMEM((8, 2, 640), f32),
            pltpu.VMEM((8, 2, 640), f32),
            pltpu.VMEM((2, 5120), f32),
            dma((4,)), dma((4,)), dma((8,)), dma((8,)), dma((2,)), dma((2,)),
            dma((7,)), dma((7,)), dma((8,)), dma((8,)),
            dma((2, 4)), dma((2, 4)), dma((2, 4)), dma((2, 4)), dma((2, 2, 2)), dma((2, 4)),
        ],
        compiler_params=pltpu.CompilerParams(
            collective_id=0, has_side_effects=True, vmem_limit_bytes=48 * 1024 * 1024
        ),
        cost_estimate=pl.CostEstimate(flops=50_000_000_000, bytes_accessed=20_000_000, transcendentals=0),
        name="gather_all",
    )(tok, shl, w, val, cot)


def scatter_kernel(
    rows, gq, qw, fish, merged,
    own_sq, sib_sq, got_sq, arrived, out, last_sq, last_got, last_arr, fin, xb, qo, wo, wi,
    s_dd, r_dd, s_rg, r_rg, s_x, r_x, s_q, r_q, s_w, r_w,
):
    m, z, x, yl, c = place()
    px, hh = lax.rem(x, 2), x // 2
    sib = (m, z, x, yl, 1 - c)
    dz = 1 - 2 * c
    znext = lax.rem(z + dz + 8, 8)
    mate = (1 - m, z, x, yl, c)
    f32, bf = jnp.float32, jnp.bfloat16

    for j in range(1, 8):
        q = lax.rem(x * 2 + c + j, 8)
        hello((m, z, q // 2, yl, lax.rem(q, 2)))
    hello((m, lax.rem(z + 1, 8), x, yl, c))
    hello((m, lax.rem(z + 7, 8), x, yl, c))
    hello(mate)
    pl.semaphore_wait(pltpu.get_barrier_semaphore(), 10)

    copy_q = remote(qw, qo, s_q, r_q, mate)
    copy_q.start()

    def squares(zs, dst):
        @pl.loop(0, 5)
        def _(r):
            cols = pl.ds(pl.multiple_of(zs * 640 + r * 128, 128), 128)
            g = lax.dot_general(
                rows[:, cols], gq[...], (((0,), (0,)), ((), ())), preferred_element_type=f32
            )
            dst[pl.ds(pl.multiple_of(r * 128, 128), 128), :] = (g * g).astype(bf)

    mine, other = pl.ds(c * HALF, HALF), pl.ds((1 - c) * HALF, HALF)

    def zat(j):
        return lax.rem(z + dz * j + 16, 8)

    def across(q):
        if q == 0:
            src, dst = own_sq.at[3, other, :], got_sq.at[3, other, :]
        elif q < 4:
            src, dst = sib_sq.at[3 - q], got_sq.at[3 - q]
        elif q == 4:
            src, dst = last_sq.at[other, :], last_got
        else:
            src, dst = arrived.at[5], last_arr
        return remote(src, dst, s_dd.at[q], r_dd.at[q], sib)

    def across_in(q):
        if q == 0:
            return remote(
                own_sq.at[3, mine, :], got_sq.at[3, mine, :], s_dd.at[q], r_dd.at[q], sib
            )
        return across(q)

    def ring(n):
        return remote(out.at[n], arrived.at[n], s_rg.at[n], r_rg.at[n], (m, znext, x, yl, c))

    def send_on(n):
        j = (8 - n) // 2 - 1
        base = (c if n % 2 == 0 else 1 - c) * HALF

        @pl.loop(0, HALF // 32)
        def _(i):
            at = pl.ds(pl.multiple_of(i * 32, 32), 32)
            far = pl.ds(pl.multiple_of(base + i * 32, 32), 32)
            total = own_sq[j, far, :].astype(f32) + got_sq[j, far, :].astype(f32)
            if n >= 2:
                total = total + arrived[n - 2, at, :].astype(f32)
            out[n, at, :] = total.astype(bf)

        ring(n).start()

    squares(zat(4), own_sq.at[3])
    across(0).start()
    squares(zat(-3), sib_sq.at[2])
    across(1).start()
    across_in(0).wait_recv()
    send_on(0)
    squares(zat(3), own_sq.at[2])
    across_in(1).wait_recv()
    send_on(1)
    squares(zat(-2), sib_sq.at[1])
    across(2).start()
    squares(zat(2), own_sq.at[1])
    ring(0).wait_recv()
    send_on(2)
    across_in(2).wait_recv()
    ring(1).wait_recv()
    send_on(3)
    squares(zat(-1), sib_sq.at[0])
    across(3).start()
    squares(zat(1), own_sq.at[0])
    ring(2).wait_recv()
    send_on(4)
    across_in(3).wait_recv()
    ring(3).wait_recv()
    send_on(5)
    squares(z, last_sq)
    across(4).start()
    ring(4).wait_recv()
    send_on(6)
    ring(5).wait_recv()
    across(5).start()
    across_in(4).wait_recv()
    across_in(5).wait_recv()
    ring(6).wait_recv()

    for u in range(2):

        @pl.loop(0, SLICE // 32)
        def _(i):
            at = pl.ds(pl.multiple_of(u * SLICE + i * 32, 32), 32)
            far = pl.ds(pl.multiple_of(c * HALF + u * SLICE + i * 32, 32), 32)
            total = last_sq[far, :].astype(f32) + last_got[at, :].astype(f32)
            total = total + arrived[6, at, :].astype(f32) + last_arr[at, :].astype(f32)
            fin[u, pl.ds(pl.multiple_of(i * 32, 32), 32), :] = total.astype(bf)

    def xs(u):
        return remote(
            fin.at[u], xb.at[hh], s_x.at[u], r_x.at[hh], (m, z, 2 * c + u, yl, px)
        )

    for u in range(2):
        own = (2 * c + u == x) & (px == c)

        @pl.when(jnp.logical_not(own))
        def _():
            xs(u).start()

        @pl.when(own)
        def _():
            xb[hh] = fin[u]

    for t in range(2):
        own = (c + 2 * t == x) & (hh == c)

        @pl.when(jnp.logical_not(own))
        def _():
            remote(fin.at[0], xb.at[t], s_x.at[0], r_x.at[t], sib).wait_recv()

    total = xb[0].astype(f32) + xb[1].astype(f32)
    fish[...] = total
    wo[...] = (total + damping).astype(bf)
    copy_w = remote(wo, wi, s_w, r_w, mate)
    copy_w.start()
    copy_q.wait_recv()
    copy_w.wait_recv()
    first = m == 0
    wa, wb = wo[...].astype(f32), wi[...].astype(f32)
    qa, qb = qw[...].astype(f32), qo[...].astype(f32)
    w0, w1 = jnp.where(first, wa, wb), jnp.where(first, wb, wa)
    q0, q1 = jnp.where(first, qa, qb), jnp.where(first, qb, qa)
    merged[...] = (w0 * q0 + w1 * q1) / (w0 + w1)

    copy_q.wait_send()
    copy_w.wait_send()
    for u in range(2):
        own = (2 * c + u == x) & (px == c)

        @pl.when(jnp.logical_not(own))
        def _():
            xs(u).wait_send()

    for n in range(7):
        ring(n).wait_send()
    for q in range(6):
        across(q).wait_send()


def scatter(rows, gq, qw):
    bf, f32 = jnp.bfloat16, jnp.float32
    vmem = pl.BlockSpec(memory_space=pltpu.VMEM)
    dma = pltpu.SemaphoreType.DMA
    return pl.pallas_call(
        scatter_kernel,
        out_shape=(
            jax.ShapeDtypeStruct((SLICE, 640), f32),
            jax.ShapeDtypeStruct((SLICE, 640), f32),
        ),
        in_specs=[vmem] * 3,
        out_specs=(vmem,) * 2,
        scratch_shapes=[
            pltpu.VMEM((4, 640, 640), bf),
            pltpu.VMEM((3, 640, 640), bf),
            pltpu.VMEM((4, 640, 640), bf),
            pltpu.VMEM((7, HALF, 640), bf),
            pltpu.VMEM((7, HALF, 640), bf),
            pltpu.VMEM((640, 640), bf),
            pltpu.VMEM((HALF, 640), bf),
            pltpu.VMEM((HALF, 640), bf),
            pltpu.VMEM((2, SLICE, 640), bf),
            pltpu.VMEM((2, SLICE, 640), bf),
            pltpu.VMEM((SLICE, 640), bf),
            pltpu.VMEM((SLICE, 640), bf),
            pltpu.VMEM((SLICE, 640), bf),
            dma((6,)), dma((6,)), dma((7,)), dma((7,)), dma((2,)), dma((2,)),
            dma, dma, dma, dma,
        ],
        compiler_params=pltpu.CompilerParams(
            collective_id=1, has_side_effects=True, vmem_limit_bytes=48 * 1024 * 1024
        ),
        cost_estimate=pl.CostEstimate(flops=30_000_000_000, bytes_accessed=20_000_000, transcendentals=0),
        name="square_scatter",
    )(rows, gq, qw)


def normed_rotation(pre, cosine, sine_table):
    halfway = pre.shape[2] // 2
    inverse = lax.rsqrt(jnp.mean(pre * pre, axis=2, keepdims=True) + 1e-06)
    normed = pre * inverse
    rotated = (
        normed * cosine[None] + jnp.roll(normed, halfway, axis=2) * sine_table[None]
    )
    return (normed, inverse, rotated.astype(jnp.bfloat16))


def on_device(tokens, lattice, timestep, time_weight, query_weight, key_weight, values, cotangent):
    member, z, x, ylo, core = place()
    f32, bf = jnp.float32, jnp.bfloat16
    features = time_features(timestep, time_weight.shape[1])
    local = jnp.einsum("cf,jfd->cjd", features, time_weight, preferred_element_type=f32)
    local = local.reshape(8, 4, 2, SLICE).transpose(1, 0, 2, 3)
    local = lax.dynamic_update_slice(
        jnp.zeros((4, 8, 2, 640), f32), local, (0, 0, 0, x * SLICE)
    )
    own_query = query_weight[0]
    own_key = lax.dynamic_slice(key_weight, (0, member * 256), (SLICE, KHEADS * HEAD_SIZE))
    both = jnp.concatenate([own_query, own_key], axis=1)

    swap = []
    for i in range(2):
        for a in range(2):
            for c in range(2):
                swap.append(((2 * i + c) * 2 + a, (2 * i + a) * 2 + c))
    grid = lax.ppermute(lattice.astype(f32), ("x", "core"), swap)
    cosine, sine_table = rope_tables(grid, HEAD_SIZE)

    rows, weights, value_heads, cot_heads = gather(tokens, local, both, values, cotangent[0])
    weights = weights.reshape(5120, 640 + KHEADS * HEAD_SIZE)

    def heads(a, count):
        return a.reshape(512, count, HEAD_SIZE).transpose(1, 0, 2)

    pre = jnp.dot(rows, weights, preferred_element_type=f32)
    key_part = normed_rotation(heads(pre[:, 640:], KHEADS), cosine, sine_table)[2]
    sent = jnp.where(member == 0, key_part[:2], key_part[1:])
    came = lax.ppermute(sent, "member", [(0, 1), (1, 0)])
    key_round = jnp.where(
        member == 0,
        jnp.concatenate([key_part, came], axis=0),
        jnp.concatenate([came, key_part], axis=0),
    )
    query_normed, query_inverse, query_round = normed_rotation(
        heads(pre[:, :640], 5), cosine, sine_table
    )
    vh, ch = heads(value_heads, 5), heads(cot_heads, 5)
    scale = HEAD_SIZE ** (-0.5)
    grad_weights = jnp.einsum("hqd,hkd->hqk", ch, vh, preferred_element_type=f32)
    scores = jnp.einsum("hqd,hkd->hqk", query_round, key_round, preferred_element_type=f32) * scale
    raised = jnp.exp(scores)
    probs = raised / jnp.sum(raised, axis=2, keepdims=True)
    attended = jnp.einsum("hqk,hkd->hqd", probs.astype(bf), vh, preferred_element_type=f32)
    inner = jnp.sum(ch.astype(f32) * attended, axis=2, keepdims=True)
    grad_scores = (probs * (grad_weights - inner)).astype(bf)
    grad_rotated = (
        jnp.einsum("hqk,hkd->hqd", grad_scores, key_round, preferred_element_type=f32) * scale
    )
    grad_normed = grad_rotated * cosine[None] + jnp.roll(
        grad_rotated * sine_table[None], HEAD_SIZE // 2, axis=2
    )
    grad_query = query_inverse * (
        grad_normed - query_normed * jnp.mean(grad_normed * query_normed, axis=2, keepdims=True)
    )
    grad_query = grad_query.transpose(1, 0, 2).reshape(512, 640).astype(bf)
    fisher, merged = scatter(rows, grad_query, own_query)
    return (fisher[None], merged)


def solution(mesh):
    finer = Mesh(mesh.devices.reshape(mesh.shape["member"], 8, 4, 2, 2), AXES)
    in_specs = (
        P(SEQ_HEAD, None),
        P(None, SEQ),
        P(),
        P(None, None, SEQ),
        P("member", SEQ, HEAD),
        P(SEQ, HEAD),
        P(SEQ_HEAD, None),
        P("member", SEQ_HEAD, None),
    )
    out_specs = (P("member", SEQ, HEAD), P(SEQ, HEAD))
    return jax.shard_map(
        on_device, mesh=finer, in_specs=in_specs, out_specs=out_specs, check_vma=False
    )
```

time: 388 us -> 202 us (0.52)
  waiting for transfers between devices: 278 us -> 6.58 us
  Pallas kernels: 0 us -> 141 us
  starting transfers between devices: 26.5 us -> 7.37 us
  between operations: 14.1 us -> 0.94 us
  matrix products: 29.1 us -> 19.4 us
  blocking collectives: 9.69 us -> 0 us
  other arithmetic: 12.4 us -> 8.3 us
    pallas_call x0 -> x2, Pallas kernels: none -> 141 us  [the longest x1 82.6 us: gather(): pl.pallas_call(gather_kernel, out_shape=(jax.ShapeDtypeStruct((512, 5120)...]
    all_gather x2 -> x0, waiting for transfers between devices: 139 us -> none  [the longest x1 118 us: side_by_side(): out = lax.all_gather(both, axis, axis=dim, tiled=True)]
    reduce_scatter x2 -> x0, waiting for transfers between devices: 100 us -> none  [own_rows(): subtotal = lax.psum_scatter(subtotal, axis, scatter_dimension=0, tiled=True)]
    all_to_all x4 -> x0, waiting for transfers between devices: 38.5 us -> none  [the longest x1 13.3 us: on_device(): lax.all_to_all(values, 'head', split_axis=1, concat_axis=0, tiled=True)]
    all_to_all x4 -> x0, starting transfers between devices: 26.3 us -> none  [the longest x1 11.9 us: on_device(): lax.all_to_all(local_shift.astype(jnp.bfloat16), SEQ, split_axis=0, conca...]
    all_to_all x1 -> x0, blocking collectives: 9.69 us -> none  [copy_for_each(): lax.all_to_all(jnp.broadcast_to(array[None], (size, *array.shape)), axis,...]
    dot_general x7 -> x5, matrix products: 29.1 us -> 19.4 us  [the longest x1 9.83 us: on_device(): pre = jnp.dot(rows, weights, preferred_element_type=f32)]
    ppermute x0 -> x2, starting transfers between devices: none -> 7.37 us  [the longest x1 4.49 us: on_device(): grid = lax.ppermute(lattice.astype(f32), ('x', 'core'), swap)]
  transfers between devices with their start and end apart: 8 -> 2, of which waited for: 8 -> 1; matrix products, arithmetic and copies ran while one was open for 3% -> 12% of each run, Pallas kernels for 0% -> 41%
where the time goes in v1:
time: 202 us; the launch traced here: 201 us
  Pallas kernels  141 us (70%)
  matrix products  19.4 us (10%)
  local copies, waits for them, and re-layouts  17.6 us (9%)
  other arithmetic  8.3 us (4%)
  starting transfers between devices  7.37 us (4%)
  waiting for transfers between devices  6.58 us (3%)
    pallas_call x1, Pallas kernels, gather(): pl.pallas_call(gather_kernel, out_shape=(jax.ShapeDtypeStruct((512, 5120)...  82.6 us
    pallas_call x1, Pallas kernels, scatter(): pl.pallas_call(scatter_kernel, out_shape=(jax.ShapeDtypeStruct((SLICE, 64...  58.7 us
    dot_general x1, matrix products, on_device(): pre = jnp.dot(rows, weights, preferred_element_type=f32)  9.83 us
    ppermute x1, waiting for transfers between devices, on_device(): came = lax.ppermute(sent, 'member', [(0, 1), (1, 0)])  6.58 us
    dot_general x1, matrix products, on_device(): jnp.einsum('hqk,hkd->hqd', grad_scores, key_round, preferred_element_type...  6.08 us
    unnamed x28, local copies, waits for them, and re-layouts  5.46 us
    ppermute x1, starting transfers between devices, on_device(): grid = lax.ppermute(lattice.astype(f32), ('x', 'core'), swap)  4.49 us
  transfers between devices with their start and end apart: 2, of which 1 were waited for; matrix products, arithmetic and copies ran while one was open for 12% of the time, Pallas kernels for 41%

profile of v1, /device:TPU:1, one launch (start us, length us, event | category | flops | bytes accessed | tf_op | source)
XLA Modules:
  0.0 201.4 jit_solution(467812629425596847)
XLA Ops:
  0.6 0.0 copy-start
  0.6 0.0 copy-start.2
  0.7 0.8 convert_element_type.72
  1.5 4.5 %collective-permute-start = (f32[3,512]{1,0:T(4,128)S(1)}, f32[3,512]{1,0:T(4,128)S(1)}, u32[]{:S(2)}, u32[]{:S(2)}) collective-permute-start(f32[3,512]{1,0:T(4,128)S(1)} %convert_element_type.72), channel_id=1, source_target_pairs={{0,0},{4,1},{1,4},{5,5},{8,8},{12,9},{9,12},{13,13},{2,2},{6,3},{3... | collective-permute-start | bytes 18440 | tf_op jit(solution)/shard_map/ppermute | solution.py:574
  6.0 0.7 convert_element_type.70
  6.7 0.1 fusion.25
  6.8 1.1 fusion.27
  7.9 0.1 copy.16
  8.0 0.0 copy-done
  8.0 1.0 pad_maximum_fusion.w
  9.0 0.7 dynamic_update_slice.3.shl
  9.7 0.0 copy-done.2
  9.7 0.0 copy-start.3
  9.7 1.1 copy-done.3
  10.8 1.1 copy-done.4
  11.9 82.6 %gather_all.1 = (bf16[512,5120]{1,0:T(8,128)(2,1)}, bf16[8,640,1024]{2,1,0:T(8,128)(2,1)}, bf16[512,640]{1,0:T(8,128)(2,1)S(1)}, bf16[512,640]{1,0:T(8,128)(2,1)S(1)}) custom-call(bf16[128,5120]{1,0:T(8,128)(2,1)S(1)} %copy-done.2, f32[4,8,2,640]{3,2,1,0:T(2,128)S(1)} %dynamic_update_slice.3.shl, bf16[160,1024]{1,0:T(8,128)(2,1)S(1)} %pad_maximum_fusion.w, ...), custom_call_target="tpu_custom_call" | custom-call | flops 49999998976 | bytes 20000000 | tf_op jit(solution)/shard_map/gather_all/pallas_call | solution.py:310
  94.5 9.8 %fusion.43 = f32[512,1024]{1,0:T(8,128)S(1)} fusion(bf16[512,5120]{1,0:T(8,128)(2,1)} %get-tuple-element.8.rows, bf16[5120,1024]{1,0:T(8,128)(2,1)} %bitcast.56), kind=kOutput, calls=%fused_computation.72 | convolution fusion | flops 5368709120 | bytes 17825792 | tf_op jit(solution)/shard_map/dot_general | solution.py:583
  104.3 1.0 slice.57
  105.3 1.2 slice.56
  106.5 1.4 copy.19
  107.9 0.0 copy-start.5
  107.9 0.1 multiply_reduce_fusion.2
  108.0 0.1 broadcast_multiply_fusion.2
  108.1 0.7 copy-done.5
  108.8 0.8 fusion.41
  109.6 1.7 copy.18
  111.3 0.2 multiply_reduce_fusion.1
  111.5 1.2 broadcast_multiply_fusion.1
  112.8 1.1 copy.22
  113.9 1.1 copy.23
  115.0 0.0 collective-permute-done
  115.0 1.9 broadcast_multiply_fusion.3
  116.9 0.3 fusion.19
  117.2 2.9 %collective-permute-start.1 = (bf16[2,512,128]{1,2,0:T(8,128)(2,1)S(1)}, bf16[2,512,128]{1,2,0:T(8,128)(2,1)S(1)}, u32[]{:S(2)}, u32[]{:S(2)}) collective-permute-start(bf16[2,512,128]{1,2,0:T(8,128)(2,1)S(1)} %slice_select_fusion), channel_id=1, source_target_pairs={{0,128},{128,0},{1,129},{129,1},{2,130},{130,2},{3,131},{131,3},{4... | collective-permute-start | bytes 786440 | tf_op jit(solution)/shard_map/ppermute | solution.py:586
  120.1 0.1 fusion.40
  120.2 6.6 %collective-permute-done.1 = bf16[2,512,128]{1,2,0:T(8,128)(2,1)S(1)} collective-permute-done((bf16[2,512,128]{1,2,0:T(8,128)(2,1)S(1)}, bf16[2,512,128]{1,2,0:T(8,128)(2,1)S(1)}, u32[]{:S(2)}, u32[]{:S(2)}) %collective-permute-start.1) | collective-permute-done | bytes 262176 | tf_op jit(solution)/shard_map/ppermute | solution.py:586
  126.8 1.2 fusion.1
  128.0 0.1 copy-done.11
  128.1 1.2 fusion.15
  129.3 1.0 copy-done.8
  130.3 6.1 %broadcast_multiply_fusion = (f32[5,512,128]{1,2,0:T(8,128)}, f32[5,512,128]{1,2,0:T(8,128)S(1)}) fusion(f32[512,128]{0,1:T(8,128)} %get-tuple-element.20, bf16[5,512,128]{1,2,0:T(8,128)(2,1)} %bitcast.47, bf16[5,512,128]{1,2,0:T(8,128)(2,1)} %bitcast.49, f32[5,512]{1,0:T(8,128)S(1)} %fusion.15, f32[5,512]{1,0:T(8,128)S(1)} %get-tuple-element.29, ...), kind=kOutput, calls=%fused_computation.24 | convolution fusion | flops 680919040 | bytes 10113025 | tf_op jit(solution)/shard_map/hqk,hkd->hqd/dot_general | solution.py:605
  136.4 1.4 fusion.39
  137.8 0.5 multiply_reduce_fusion
  138.4 1.4 multiply_convert_fusion.2
  139.8 1.4 copy.25.gq
  141.2 58.7 %square_scatter.1 = (f32[160,640]{1,0:T(8,128)S(1)}, f32[160,640]{1,0:T(8,128)S(1)}) custom-call(bf16[512,5120]{1,0:T(8,128)(2,1)} %get-tuple-element.8.rows, bf16[512,640]{1,0:T(8,128)(2,1)S(1)} %copy.25.gq, bf16[160,640]{1,0:T(8,128)(2,1)S(1)} %bitcast.37), custom_call_target="tpu_custom_call" | custom-call | flops 30000001024 | bytes 20000000 | tf_op jit(solution)/shard_map/square_scatter/pallas_call | solution.py:513
  199.9 0.8 copy.34
  200.7 0.8 copy.35
  (26 shorter events, 0.2 us)
Async XLA Ops:
  0.6 7.3 %copy-start = (bf16[160,640]{1,0:T(8,128)(2,1)S(1)}, bf16[160,640]{1,0:T(8,128)(2,1)}, u32[]{:S(2)}) copy-start(bf16[160,640]{1,0:T(8,128)(2,1)} %param.13) | copy-start | bytes 614404
  0.6 9.1 %copy-start.2 = (bf16[128,5120]{1,0:T(8,128)(2,1)S(1)}, bf16[128,5120]{1,0:T(8,128)(2,1)}, u32[]{:S(2)}) copy-start(bf16[128,5120]{1,0:T(8,128)(2,1)} %tok.1) | copy-start | bytes 3932164
  1.5 113.5 %collective-permute-start = (f32[3,512]{1,0:T(4,128)S(1)}, f32[3,512]{1,0:T(4,128)S(1)}, u32[]{:S(2)}, u32[]{:S(2)}) collective-permute-start(f32[3,512]{1,0:T(4,128)S(1)} %convert_element_type.72), channel_id=1, source_target_pairs={{0,0},{4,1},{1,4},{5,5},{8,8},{12,9},{9,12},{13,13},{2,2},{6,3},{3... | collective-permute-start | bytes 18440 | tf_op jit(solution)/shard_map/ppermute | solution.py:574
  9.7 1.1 copy-start.3
  10.8 1.1 copy-start.4
  107.9 0.9 copy-start.5
  113.9 3.0 %copy-start.9 = (f32[3,512,64]{1,2,0:T(8,128)S(1)}, f32[3,512,64]{1,2,0:T(8,128)}, u32[]{:S(2)}) copy-start(f32[3,512,64]{1,2,0:T(8,128)} %get-tuple-element.19) | copy-start | bytes 1179652
  115.0 1.9 copy-start.6
  116.9 3.2 %copy-start.7 = (f32[5,512,128]{1,2,0:T(8,128)S(1)}, f32[5,512,128]{1,2,0:T(8,128)}, u32[]{:S(2)}) copy-start(f32[5,512,128]{1,2,0:T(8,128)} %broadcast_multiply_fusion.1) | copy-start | bytes 3932164
  117.2 9.6 %collective-permute-start.1 = (bf16[2,512,128]{1,2,0:T(8,128)(2,1)S(1)}, bf16[2,512,128]{1,2,0:T(8,128)(2,1)S(1)}, u32[]{:S(2)}, u32[]{:S(2)}) collective-permute-start(bf16[2,512,128]{1,2,0:T(8,128)(2,1)S(1)} %slice_select_fusion), channel_id=1, source_target_pairs={{0,128},{128,0},{1,129},{129,1},{2,130},{130,2},{3,131},{131,3},{4... | collective-permute-start | bytes 786440 | tf_op jit(solution)/shard_map/ppermute | solution.py:586
  126.8 1.2 copy-start.12
  126.8 1.3 copy-start.10
  126.8 1.4 copy-start.11
  128.0 2.3 %copy-start.8 = (f32[5,512,512]{1,2,0:T(8,128)}, f32[5,512,512]{1,2,0:T(8,128)S(1)}, u32[]{:S(2)}) copy-start(f32[5,512,512]{1,2,0:T(8,128)S(1)} %get-tuple-element.30) | copy-start | bytes 15728644
  139.8 1.4 copy-start.1

commit v2 on v0

v2 whole, which is shorter than its diff:
```python
import math

import jax
import jax.numpy as jnp
from jax import lax
from jax.experimental import pallas as pl
from jax.experimental.pallas import tpu as pltpu
from jax.sharding import Mesh
from jax.sharding import PartitionSpec as P

HEAD_SIZE = 128
AXES = ("member", "z", "x", "ylo", "core")
SEQ = ("z", "x")
HEAD = ("ylo", "core")
SEQ_HEAD = ("z", "x", "ylo", "core")
MESH = pl.DeviceIdType.MESH

damping = 0.01
SLICE = 160
HALF = 320
KW = 384
ROW_CHUNK = 32
BLOCK = 128
F32, BF = jnp.float32, jnp.bfloat16


def place():
    return tuple(lax.axis_index(a) for a in AXES)


def remote(src, dst, send, recv, to):
    return pltpu.make_async_remote_copy(
        src_ref=src, dst_ref=dst, send_sem=send, recv_sem=recv, device_id=to, device_id_type=MESH
    )


def hello(to):
    pl.semaphore_signal(pltpu.get_barrier_semaphore(), inc=1, device_id=to, device_id_type=MESH)


def rope_frequency():
    halfway, side = HEAD_SIZE // 2, HEAD_SIZE // 6
    frame = halfway - 2 * side
    shape = (8, HEAD_SIZE)
    row = lax.broadcasted_iota(jnp.int32, shape, 0)
    column = lax.broadcasted_iota(jnp.int32, shape, 1)
    pair = jnp.where(column < halfway, column, column - halfway)
    axis = jnp.where(pair < frame, 0, jnp.where(pair < frame + side, 1, 2))
    anchor = jnp.where(axis == 0, 0, jnp.where(axis == 1, frame, frame + side))
    span = jnp.where(axis == 0, frame, side).astype(F32)
    frequency = jnp.exp(-math.log(10000.0) * (pair - anchor).astype(F32) / span)
    return jnp.where(row == axis, frequency, 0.0)


def kernel(
    when, tw, lat, tok_hbm, wq_hbm, wk_hbm, val, cot,
    xb, wo, wi, qo, wqv,
    tok, wkv, bigq, bigk, rows, vals, cots, made,
    ang, wide, shl, buf1, tot, buf2, mod, latb, latf, cosb, sinb,
    qacc, kacc, krot, gq,
    own_sq, sib_sq, got_sq, arrived, out, last_sq, last_got, last_arr, fin,
    s_in, s_self, s_l, r_l,
    s_m1, r_m1, s_m2, r_m2, s_s1, r_s1, s_rg, r_rg, s_dd, r_dd,
    s_r1, r_r1, s_r2, r_r2, s_v, r_v, s_k, r_k,
    s_sd, r_sd, s_sr, r_sr, s_x, r_x, s_q, r_q, s_w, r_w,
):
    m, z, x, yl, c = place()
    px, pair, hh = lax.rem(x, 2), x // 2, x // 2
    sib = (m, z, x, yl, 1 - c)
    mate = (1 - m, z, x, yl, c)
    dz = 1 - 2 * c
    znext = lax.rem(z + dz + 8, 8)
    home = c == px
    up = (jnp.where(yl == 0, m, 1 - m), z, x, 1 - yl, c)
    down = (jnp.where(yl == 0, 1 - m, m), z, x, 1 - yl, c)
    away = jnp.logical_not(home)

    loads = [
        pltpu.make_async_copy(wk_hbm.at[:, pl.ds(pl.multiple_of(m * 256, 128), KW)], wkv, s_in.at[0]),
        pltpu.make_async_copy(wq_hbm, wqv, s_in.at[1]),
        pltpu.make_async_copy(tok_hbm, tok, s_in.at[2]),
    ]
    for load in loads:
        load.start()

    for j in range(1, 16):
        q = lax.rem(x * 4 + yl * 2 + c + j, 16)
        hello((m, z, q // 4, lax.rem(q, 4) // 2, lax.rem(q, 2)))
    for j in range(1, 8):
        hello((m, lax.rem(z + j, 8), x, yl, c))
    hello((1 - m, z, x, 1 - yl, c))
    hello(mate)

    ladder = lax.broadcasted_iota(jnp.int32, (1, 128), 1).astype(F32)
    frequency = jnp.exp(-math.log(10000.0) * 2.0 * ladder / 256)
    for a in range(4):
        for b in range(8):
            r = a * 8 + b
            ang[r : r + 1, :] = when[b * 4 + a].astype(F32) * frequency
    for j in range(2):
        wide[j] = jnp.zeros((640, 256), BF)
        wide[j, pl.ds(pl.multiple_of(x * SLICE, SLICE), SLICE), :] = tw[j]
    angle = ang[...]
    feature = jnp.concatenate([jnp.cos(angle), jnp.sin(angle)], axis=1).astype(BF)
    for j in range(2):
        part = lax.dot_general(
            feature, wide[j], (((1,), (1,)), ((), ())), preferred_element_type=F32
        )
        for a in range(4):
            shl[a, j] = part[a * 8 : (a + 1) * 8, :]
    for load in loads[:2]:
        load.wait()

    pl.semaphore_wait(pltpu.get_barrier_semaphore(), 24)

    def m1(j):
        to = lax.rem(x + j, 4)
        return remote(shl.at[to], buf1.at[x], s_m1.at[j], r_m1.at[j], (m, z, to, yl, c))

    for j in range(1, 4):
        m1(j).start()

    def s1(a, t):
        src, dst = ((wkv, bigk), (wqv, bigq))[a]
        return remote(
            src, dst.at[z, pl.ds(x * SLICE, SLICE), :], s_s1.at[a, t],
            r_s1.at[a, lax.rem(x, 2)], (m, z, c + 2 * t, yl, hh),
        )

    for a in range(2):
        for t in range(2):
            own = (c + 2 * t == x) & (hh == c)

            @pl.when(jnp.logical_not(own))
            def _():
                s1(a, t).start()

            @pl.when(own)
            def _():
                src, dst = ((wkv, bigk), (wqv, bigq))[a]
                dst[z, pl.ds(pl.multiple_of(x * SLICE, SLICE), SLICE), :] = src[...]

    send_lat = remote(lat, latb, s_l, r_l, (m, z, 2 * pair + 1 - px, yl, px))

    @pl.when(home)
    def _():
        latf[...] = jnp.zeros((8, 512), F32)
        latf[0:3, :] = lat[...].astype(F32)

    @pl.when(home)
    def _():
        send_lat.start()

    buf1[x] = shl[x]
    for j in range(1, 4):
        m1(j).wait_recv()
    total = buf1[0] + buf1[1] + buf1[2] + buf1[3]
    for k in range(8):
        for j in range(2):
            tot[k, j : j + 1, :] = total[j, k : k + 1, :]

    def m2(j):
        to = lax.rem(z + j, 8)
        return remote(tot.at[to], buf2.at[z], s_m2.at[j], r_m2.at[j], (m, to, x, yl, c))

    for j in range(1, 8):
        m2(j).start()
    buf2[z] = tot[z]

    def half_of(n):
        return c if n % 2 == 0 else 1 - c

    def ring(a, n):
        origin = lax.rem(z - dz * (n // 2) + 8, 8)
        spot = (bigk, bigq)[a].at[origin, pl.ds(half_of(n) * HALF, HALF), :]
        return remote(spot, spot, s_rg.at[a, n], r_rg.at[a, n], (m, znext, x, yl, c))

    def across(a, n):
        k = n - 1
        big = (bigk, bigq)[a]
        if n == 0:
            spot = big.at[z, pl.ds(c * HALF, HALF), :]
        else:
            origin = lax.rem(z - dz * (k // 2 + 1) + 8, 8)
            spot = big.at[origin, pl.ds(half_of(k) * HALF, HALF), :]
        return remote(spot, spot, s_dd.at[a, n], r_dd.at[a, n], sib)

    def s1_arrived(a):
        for u in range(2):
            own = (2 * c + u == x) & home

            @pl.when(jnp.logical_not(own))
            def _():
                src, dst = ((wkv, bigk), (wqv, bigq))[a]
                remote(
                    src, dst.at[z, pl.ds((2 * c + u) * SLICE, SLICE), :],
                    s_s1.at[a, 0], r_s1.at[a, u], sib,
                ).wait_recv()

    for a in range(2):
        s1_arrived(a)
        ring(a, 0).start()
        across(a, 0).start()

    @pl.when(away)
    def _():
        send_lat.wait_recv()
        latf[...] = jnp.zeros((8, 512), F32)
        latf[0:3, :] = latb[...].astype(F32)

    for j in range(1, 8):
        m2(j).wait_recv()
    for k in range(8):
        mod[:, k * 640 : (k + 1) * 640] = buf2[k]
    loads[2].wait()

    def r1(t, k):
        return remote(
            made.at[pl.ds(k * ROW_CHUNK, ROW_CHUNK), :],
            rows.at[pl.ds((2 * yl + c) * 128 + k * ROW_CHUNK, ROW_CHUNK), :],
            s_r1.at[t, k], r_r1.at[c, k], (m, z, 2 * pair + t, yl, px),
        )

    for k in range(4):

        @pl.loop(0, ROW_CHUNK // 16)
        def _(i):
            at = pl.multiple_of(k * ROW_CHUNK + i * 16, 16)
            hidden = tok[pl.ds(at, 16), :].astype(F32)
            average = jnp.mean(hidden, axis=1, keepdims=True)
            centred = hidden - average
            variance = jnp.mean(centred * centred, axis=1, keepdims=True)
            normed = centred * lax.rsqrt(variance + 1e-06)
            made[pl.ds(at, 16), :] = (normed * (1.0 + mod[1:2, :]) + mod[0:1, :]).astype(BF)

        for t in range(2):
            own = (2 * pair + t == x) & home

            @pl.when(jnp.logical_not(own))
            def _():
                r1(t, k).start()

            @pl.when(own)
            def _():
                at = pl.multiple_of((2 * yl + c) * 128 + k * ROW_CHUNK, ROW_CHUNK)
                rows[pl.ds(at, ROW_CHUNK), :] = made[k * ROW_CHUNK : (k + 1) * ROW_CHUNK, :]

    for a in range(2):
        across(a, 0).wait_recv()
        ring(a, 1).start()

    def share(a, t, y2):
        h2 = 2 * y2 + t
        src, dst = ((val, vals), (cot, cots))[a]
        return remote(
            src.at[:, h2 * 640 : (h2 + 1) * 640],
            dst.at[pl.ds((2 * yl + c) * 128, 128), :],
            s_v.at[a, t, y2], r_v.at[a, 2 * yl + c], (m, z, 2 * pair + t, y2, px),
        )

    def keep(a):
        src, dst = ((val, vals), (cot, cots))[a]
        return pltpu.make_async_copy(
            src.at[:, pl.ds(pl.multiple_of((2 * yl + px) * 640, 128), 640)],
            dst.at[pl.ds((2 * yl + c) * 128, 128), :],
            s_self.at[a],
        )

    for t in range(2):
        for y2 in range(2):
            own = (2 * pair + t == x) & (y2 == yl) & home

            @pl.when(jnp.logical_not(own))
            def _():
                share(1, t, y2).start()
                share(0, t, y2).start()

    @pl.when(home)
    def _():
        keep(0).start()
        keep(1).start()

    copy_q = remote(wqv, qo, s_q, r_q, mate)
    copy_q.start()

    @pl.loop(0, 4)
    def _(i):
        at = pl.multiple_of(i * BLOCK, BLOCK)
        angles = lax.dot_general(
            latf[:, pl.ds(at, BLOCK)], rope_frequency(), (((0,), (0,)), ((), ())),
            precision=lax.Precision.HIGHEST, preferred_element_type=F32,
        )
        column = lax.broadcasted_iota(jnp.int32, (BLOCK, HEAD_SIZE), 1)
        cosb[pl.ds(at, BLOCK), :] = jnp.cos(angles)
        sine = jnp.sin(angles)
        sinb[pl.ds(at, BLOCK), :] = jnp.where(column < HEAD_SIZE // 2, -sine, sine)

    def r2(p, k, ylo):
        spot = rows.at[pl.ds((2 * ylo + p) * 128 + k * ROW_CHUNK, ROW_CHUNK), :]
        return remote(spot, spot, s_r2.at[p, k], r_r2.at[p, k], up if p == 0 else down)

    def ring_step(n):
        for a in range(2):
            ring(a, n).wait_recv()
            if n + 2 < 7:
                ring(a, n + 2).start()
            across(a, n + 1).start()

    for k in range(4):
        for p in range(2):
            own = home & (c == p)

            @pl.when(jnp.logical_not(own))
            def _():
                spot = rows.at[pl.ds((2 * yl + p) * 128 + k * ROW_CHUNK, ROW_CHUNK), :]
                remote(
                    made.at[pl.ds(k * ROW_CHUNK, ROW_CHUNK), :],
                    spot, s_r1.at[0, k], r_r1.at[p, k], sib,
                ).wait_recv()

            r2(p, k, yl).start()
        ring_step(k)

    for k in range(4):
        for p in range(2):
            r2(p, k, 1 - yl).wait_recv()

    def project(a, zo, first):
        acc, big = ((kacc, bigk), (qacc, bigq))[a]
        cols = pl.ds(pl.multiple_of(zo * 640, 128), 640)

        @pl.loop(0, acc.shape[1] // 128)
        def _(i):
            lanes = pl.ds(pl.multiple_of(i * 128, 128), 128)
            term = jnp.dot(rows[:, cols], big[zo, :, lanes], preferred_element_type=F32)
            if first:
                acc[:, lanes] = term
            else:
                acc[:, lanes] = acc[:, lanes] + term

    def at_distance(d):
        return lax.rem(z + d + 8, 8)

    ring_step(4)
    for a in range(2):
        project(a, z, True)
    for n in range(1, 5):
        for a in range(2):
            across(a, n).wait_recv()
    for d in (1, -1, 2, -2):
        for a in range(2):
            project(a, at_distance(d), False)
    ring_step(5)
    for n in (5, 6):
        for a in range(2):
            across(a, n).wait_recv()
    for d in (3, -3):
        for a in range(2):
            project(a, at_distance(d), False)

    def last_step(a):
        ring(a, 6).wait_recv()
        across(a, 7).start()
        across(a, 7).wait_recv()
        project(a, at_distance(4), False)

    def turned(pre, at):
        inverse = lax.rsqrt(jnp.mean(pre * pre, axis=1, keepdims=True) + 1e-06)
        normed = pre * inverse
        rotated = normed * cosb[at, :] + pltpu.roll(normed, HEAD_SIZE // 2, 1) * sinb[at, :]
        return inverse, normed, rotated.astype(BF)

    last_step(0)

    @pl.loop(0, 4)
    def _(i):
        at = pl.ds(pl.multiple_of(i * BLOCK, BLOCK), BLOCK)
        for j in range(3):
            lanes = pl.ds(pl.multiple_of((2 * m + j) * 128, 128), 128)
            krot[at, lanes] = turned(kacc[at, j * 128 : (j + 1) * 128], at)[2]

    def keys(who):
        spot = krot.at[:, pl.ds(pl.multiple_of(who * KW, 128), 256)]
        return remote(spot, spot, s_k, r_k, mate)

    keys(m).start()
    last_step(1)

    for hd in range(4):
        own = home & (hd == 2 * yl + c)

        @pl.when(jnp.logical_not(own))
        def _():
            for a, (src, dst) in enumerate(((val, vals), (cot, cots))):
                remote(
                    src.at[:, 0:640], dst.at[hd * 128 : (hd + 1) * 128, :],
                    s_v.at[a, 0, 0], r_v.at[a, hd], sib,
                ).wait_recv()

    @pl.when(home)
    def _():
        keep(0).wait()
        keep(1).wait()

    scale = HEAD_SIZE ** (-0.5)

    def attend(first, count):
        @pl.loop(0, 4 * count)
        def _(i):
            lanes = pl.ds(pl.multiple_of((first + i // 4) * 128, 128), 128)
            at = pl.ds(pl.multiple_of(lax.rem(i, 4) * BLOCK, BLOCK), BLOCK)
            inverse, normed, query = turned(qacc[at, lanes], at)
            key, value = krot[:, lanes], vals[:, lanes]
            nt = (((1,), (1,)), ((), ()))
            scores = lax.dot_general(query, key, nt, preferred_element_type=F32)
            raised = jnp.exp2(scores * (scale * math.log2(math.e)))
            probs = raised / jnp.sum(raised, axis=1, keepdims=True)
            grad_probs = lax.dot_general(cots[at, lanes], value, nt, preferred_element_type=F32)
            inner = jnp.sum(probs * grad_probs, axis=1, keepdims=True)
            grad_scores = (probs * (grad_probs - inner)).astype(BF)
            turn = jnp.dot(grad_scores, key, preferred_element_type=F32) * scale
            grad = turn * cosb[at, :] + pltpu.roll(turn * sinb[at, :], HEAD_SIZE // 2, 1)
            mean = jnp.mean(grad * normed, axis=1, keepdims=True)
            gq[at, lanes] = (inverse * (grad - normed * mean)).astype(BF)

    attend(2 * m, 3)
    keys(1 - m).wait_recv()
    attend(3 - 3 * m, 2)

    def squares(zs, dst):
        @pl.loop(0, 5)
        def _(r):
            cols = pl.ds(pl.multiple_of(zs * 640 + r * 128, 128), 128)
            g = lax.dot_general(
                rows[:, cols], gq[...], (((0,), (0,)), ((), ())), preferred_element_type=F32
            )
            dst[pl.ds(pl.multiple_of(r * 128, 128), 128), :] = (g * g).astype(BF)

    mine, other = pl.ds(c * HALF, HALF), pl.ds((1 - c) * HALF, HALF)

    def zat(j):
        return lax.rem(z + dz * j + 16, 8)

    def pass_on(q):
        if q == 0:
            src, dst = own_sq.at[3, other, :], got_sq.at[3, other, :]
        elif q < 4:
            src, dst = sib_sq.at[3 - q], got_sq.at[3 - q]
        elif q == 4:
            src, dst = last_sq.at[other, :], last_got
        else:
            u = q - 5
            src, dst = arrived.at[5, u], last_arr.at[u]
        return remote(src, dst, s_sd.at[q], r_sd.at[q], sib)

    def passed(q):
        if q == 0:
            return remote(
                own_sq.at[3, mine, :], got_sq.at[3, mine, :], s_sd.at[q], r_sd.at[q], sib
            )
        return pass_on(q)

    def sums(n, u):
        return remote(out.at[n, u], arrived.at[n, u], s_sr.at[n, u], r_sr.at[n, u], (m, znext, x, yl, c))

    def send_on(n):
        j = (8 - n) // 2 - 1
        base = (c if n % 2 == 0 else 1 - c) * HALF
        for u in range(2):
            if n >= 2:
                sums(n - 2, u).wait_recv()

            @pl.loop(0, SLICE // 32)
            def _(i):
                at = pl.ds(pl.multiple_of(i * 32, 32), 32)
                far = pl.ds(pl.multiple_of(base + u * SLICE + i * 32, 32), 32)
                total = own_sq[j, far, :].astype(F32) + got_sq[j, far, :].astype(F32)
                if n >= 2:
                    total = total + arrived[n - 2, u, at, :].astype(F32)
                out[n, u, at, :] = total.astype(BF)

            sums(n, u).start()

    squares(zat(4), own_sq.at[3])
    pass_on(0).start()
    squares(zat(-3), sib_sq.at[2])
    pass_on(1).start()
    passed(0).wait_recv()
    send_on(0)
    squares(zat(3), own_sq.at[2])
    passed(1).wait_recv()
    send_on(1)
    squares(zat(-2), sib_sq.at[1])
    pass_on(2).start()
    squares(zat(2), own_sq.at[1])
    send_on(2)
    passed(2).wait_recv()
    send_on(3)
    squares(zat(-1), sib_sq.at[0])
    pass_on(3).start()
    squares(zat(1), own_sq.at[0])
    send_on(4)
    passed(3).wait_recv()
    send_on(5)
    squares(z, last_sq)
    pass_on(4).start()
    send_on(6)

    def xs(u):
        return remote(fin.at[u], xb.at[hh], s_x.at[u], r_x.at[hh], (m, z, 2 * c + u, yl, px))

    for u in range(2):
        sums(5, u).wait_recv()
        pass_on(5 + u).start()
    passed(4).wait_recv()
    for u in range(2):
        passed(5 + u).wait_recv()
        sums(6, u).wait_recv()

        @pl.loop(0, SLICE // 32)
        def _(i):
            at = pl.ds(pl.multiple_of(i * 32, 32), 32)
            near = pl.ds(pl.multiple_of(u * SLICE + i * 32, 32), 32)
            far = pl.ds(pl.multiple_of(c * HALF + u * SLICE + i * 32, 32), 32)
            total = last_sq[far, :].astype(F32) + last_got[near, :].astype(F32)
            total = total + arrived[6, u, at, :].astype(F32) + last_arr[u, at, :].astype(F32)
            fin[u, at, :] = total.astype(BF)

        own = (2 * c + u == x) & home

        @pl.when(jnp.logical_not(own))
        def _():
            xs(u).start()

        @pl.when(own)
        def _():
            xb[hh] = fin[u]

    for t in range(2):
        own = (c + 2 * t == x) & (hh == c)

        @pl.when(jnp.logical_not(own))
        def _():
            remote(fin.at[0], xb.at[t], s_x.at[0], r_x.at[t], sib).wait_recv()

    wo[...] = (xb[0].astype(F32) + xb[1].astype(F32) + damping).astype(BF)
    copy_w = remote(wo, wi, s_w, r_w, mate)
    copy_w.start()

    for j in range(1, 4):
        m1(j).wait_send()
    for j in range(1, 8):
        m2(j).wait_send()

    @pl.when(home)
    def _():
        send_lat.wait_send()

    for t in range(2):
        own = (c + 2 * t == x) & (hh == c)

        @pl.when(jnp.logical_not(own))
        def _():
            for a in range(2):
                s1(a, t).wait_send()

        own_r = (2 * pair + t == x) & home

        @pl.when(jnp.logical_not(own_r))
        def _():
            for k in range(4):
                r1(t, k).wait_send()

        for y2 in range(2):
            own_v = (2 * pair + t == x) & (y2 == yl) & home

            @pl.when(jnp.logical_not(own_v))
            def _():
                share(0, t, y2).wait_send()
                share(1, t, y2).wait_send()

    for a in range(2):
        for n in range(7):
            ring(a, n).wait_send()
        for n in range(8):
            across(a, n).wait_send()
    for k in range(4):
        for p in range(2):
            r2(p, k, yl).wait_send()
    keys(m).wait_send()
    for n in range(7):
        for u in range(2):
            sums(n, u).wait_send()
    for q in range(7):
        pass_on(q).wait_send()
    for u in range(2):
        own = (2 * c + u == x) & home

        @pl.when(jnp.logical_not(own))
        def _():
            xs(u).wait_send()

    copy_q.wait()
    copy_w.wait()


def step(timestep, tw, lattice, tokens, own_query, own_key, values, cotangent):
    vmem = pl.BlockSpec(memory_space=pltpu.VMEM)
    hbm = pl.BlockSpec(memory_space=pl.ANY)
    dma = pltpu.SemaphoreType.DMA

    def v(shape, dtype=BF):
        return pltpu.VMEM(shape, dtype)

    return pl.pallas_call(
        kernel,
        out_shape=(
            jax.ShapeDtypeStruct((2, SLICE, 640), BF),
            jax.ShapeDtypeStruct((SLICE, 640), BF),
            jax.ShapeDtypeStruct((SLICE, 640), BF),
            jax.ShapeDtypeStruct((SLICE, 640), BF),
            jax.ShapeDtypeStruct((SLICE, 640), BF),
        ),
        in_specs=[pl.BlockSpec(memory_space=pltpu.SMEM), vmem, vmem] + [hbm] * 5,
        out_specs=(vmem,) * 5,
        scratch_shapes=[
            v((128, 5120)), v((SLICE, KW)), v((8, 640, 640)), v((8, 640, KW)),
            v((512, 5120)), v((512, 640)), v((512, 640)), v((128, 5120)),
            v((32, 128), F32), v((2, 640, 256)), v((4, 2, 8, 640), F32), v((4, 2, 8, 640), F32),
            v((8, 2, 640), F32), v((8, 2, 640), F32), v((2, 5120), F32),
            v((3, 512), jnp.int32), v((8, 512), F32), v((512, 128), F32), v((512, 128), F32),
            v((512, 640), F32), v((512, KW), F32), v((512, 640)), v((512, 640)),
            v((4, 640, 640)), v((3, 640, 640)), v((4, 640, 640)),
            v((7, 2, SLICE, 640)), v((7, 2, SLICE, 640)),
            v((640, 640)), v((HALF, 640)), v((2, SLICE, 640)), v((2, SLICE, 640)),
            dma((3,)), dma((2,)), dma, dma,
            dma((4,)), dma((4,)), dma((8,)), dma((8,)), dma((2, 2)), dma((2, 2)),
            dma((2, 7)), dma((2, 7)), dma((2, 8)), dma((2, 8)),
            dma((2, 4)), dma((2, 4)), dma((2, 4)), dma((2, 4)), dma((2, 2, 2)), dma((2, 4)),
            dma, dma,
            dma((7,)), dma((7,)), dma((7, 2)), dma((7, 2)), dma((2,)), dma((2,)),
            dma, dma, dma, dma,
        ],
        compiler_params=pltpu.CompilerParams(
            collective_id=0, has_side_effects=True, vmem_limit_bytes=60 * 1024 * 1024
        ),
        name="fisher_step",
    )(timestep, tw, lattice, tokens, own_query, own_key, values, cotangent)


def on_device(tokens, lattice, timestep, time_weight, query_weight, key_weight, values, cotangent):
    member = lax.axis_index("member")
    xb, wo, wi, qo, mine = step(
        timestep, time_weight.transpose(0, 2, 1), lattice, tokens,
        query_weight[0], key_weight, values, cotangent[0],
    )
    fisher = xb[0].astype(F32) + xb[1].astype(F32)
    first = member == 0
    w0, w1 = jnp.where(first, wo, wi).astype(F32), jnp.where(first, wi, wo).astype(F32)
    q0, q1 = jnp.where(first, mine, qo).astype(F32), jnp.where(first, qo, mine).astype(F32)
    return (fisher[None], (w0 * q0 + w1 * q1) / (w0 + w1))


def solution(mesh):
    finer = Mesh(mesh.devices.reshape(mesh.shape["member"], 8, 4, 2, 2), AXES)
    in_specs = (
        P(SEQ_HEAD, None),
        P(None, SEQ),
        P(),
        P(None, None, SEQ),
        P("member", SEQ, HEAD),
        P(SEQ, HEAD),
        P(SEQ_HEAD, None),
        P("member", SEQ_HEAD, None),
    )
    out_specs = (P("member", SEQ, HEAD), P(SEQ, HEAD))
    return jax.shard_map(
        on_device, mesh=finer, in_specs=in_specs, out_specs=out_specs, check_vma=False
    )
```

time: 388 us -> 173 us (0.45)
  waiting for transfers between devices: 278 us -> 0 us
  Pallas kernels: 0 us -> 168 us
  matrix products: 29.1 us -> 0 us
  starting transfers between devices: 26.5 us -> 0 us
  local copies, waits for them, and re-layouts: 14.4 us -> 0 us
  between operations: 14.1 us -> 0.65 us
  blocking collectives: 9.69 us -> 0 us
  other arithmetic: 12.4 us -> 4 us
    pallas_call x0 -> x1, Pallas kernels: none -> 168 us  [step(): pl.pallas_call(kernel, out_shape=(jax.ShapeDtypeStruct((2, SLICE, 640), B...]
    all_gather x2 -> x0, waiting for transfers between devices: 139 us -> none  [the longest x1 118 us: side_by_side(): out = lax.all_gather(both, axis, axis=dim, tiled=True)]
    reduce_scatter x2 -> x0, waiting for transfers between devices: 100 us -> none  [own_rows(): subtotal = lax.psum_scatter(subtotal, axis, scatter_dimension=0, tiled=True)]
    all_to_all x4 -> x0, waiting for transfers between devices: 38.5 us -> none  [the longest x1 13.3 us: on_device(): lax.all_to_all(values, 'head', split_axis=1, concat_axis=0, tiled=True)]
    dot_general x7 -> x0, matrix products: 29.1 us -> none  [the longest x2 14.4 us: contract(): return jnp.dot(clip_rows, portion, preferred_element_type=jnp.float32)]
    all_to_all x4 -> x0, starting transfers between devices: 26.3 us -> none  [the longest x1 11.9 us: on_device(): lax.all_to_all(local_shift.astype(jnp.bfloat16), SEQ, split_axis=0, conca...]
    all_to_all x1 -> x0, blocking collectives: 9.69 us -> none  [copy_for_each(): lax.all_to_all(jnp.broadcast_to(array[None], (size, *array.shape)), axis,...]
    unnamed x38 -> x0, local copies, waits for them, and re-layouts: 7.86 us -> none
  transfers between devices with their start and end apart: 8 -> 0, of which waited for: 8 -> 0; matrix products, arithmetic and copies ran while one was open for 3% -> 0% of each run, Pallas kernels for 0% -> 0%
where the time goes in v2:
time: 173 us
  Pallas kernels  168 us (97%)
  other arithmetic  4 us (2%)
    pallas_call x1, Pallas kernels, step(): pl.pallas_call(kernel, out_shape=(jax.ShapeDtypeStruct((2, SLICE, 640), B...  168 us

profile of v2, /device:TPU:1, one launch (start us, length us, event | category | flops | bytes accessed | tf_op | source)
XLA Modules:
  0.0 172.9 jit_solution(11661057126268294577)
XLA Ops:
  0.6 168.2 %fisher_step.1 = (bf16[2,160,640]{2,1,0:T(8,128)(2,1)}, bf16[160,640]{1,0:T(8,128)(2,1)}, bf16[160,640]{1,0:T(8,128)(2,1)}, bf16[160,640]{1,0:T(8,128)(2,1)}, bf16[160,640]{1,0:T(8,128)(2,1)}) custom-call(s32[32]{0:T(128)} %when.1, bf16[2,160,256]{2,1,0:T(8,128)(2,1)} %bitcast.5, s32[3,512]{1,0:T(4,128)} %lat.1, bf16[128,5120]{1,0:T(8,128)(2,1)} %tok_hbm.1, ...), custom_call_target="tpu_custom_call" | custom-call | tf_op jit(solution)/shard_map/fisher_step/pallas_call | solution.py:615
  168.9 1.8 %convert_add_fusion.1 = f32[1,160,640]{2,1,0:T(8,128)} fusion(bf16[2,160,640]{2,1,0:T(8,128)(2,1)} %get-tuple-element.7), kind=kLoop, calls=%fused_computation.5 | loop fusion | flops 307200 | bytes 819200 | tf_op jit(solution)/shard_map/add | solution.py:657
  170.7 2.2 %fusion.1 = f32[160,640]{1,0:T(8,128)} fusion(bf16[160,640]{1,0:T(8,128)(2,1)} %get-tuple-element.11, bf16[160,640]{1,0:T(8,128)(2,1)} %get-tuple-element.10, bf16[160,640]{1,0:T(8,128)(2,1)} %get-tuple-element.9, bf16[160,640]{1,0:T(8,128)(2,1)} %get-tuple-element.8, pred[]{:T(512)S(6)} %eq.3), kind=kLoop, calls=%fused_computation.4 | loop fusion | flops 1331200 | bytes 1228801 | tf_op jit(solution)/shard_map/div | solution.py:661

commit v3 on v2

--- a/solution.py
+++ b/solution.py
@@ -21,6 +21,7 @@
 KW = 384
 ROW_CHUNK = 32
 BLOCK = 128
+QUERY = 256
 F32, BF = jnp.float32, jnp.bfloat16
 
 
@@ -58,7 +59,8 @@
     tok, wkv, bigq, bigk, rows, vals, cots, made,
     ang, wide, shl, buf1, tot, buf2, mod, latb, latf, cosb, sinb,
     qacc, kacc, krot, gq,
-    own_sq, sib_sq, got_sq, arrived, out, last_sq, last_got, last_arr, fin,
+    own_a, sib_a, got_a, arr_a, out_a, last_a, lgot_a, larr_a, fin_a,
+    own_b, sib_b, got_b, arr_b, out_b, last_b, lgot_b, larr_b, fin_b,
     s_in, s_self, s_l, r_l,
     s_m1, r_m1, s_m2, r_m2, s_s1, r_s1, s_rg, r_rg, s_dd, r_dd,
     s_r1, r_r1, s_r2, r_r2, s_v, r_v, s_k, r_k,
@@ -127,18 +129,23 @@
             r_s1.at[a, lax.rem(x, 2)], (m, z, c + 2 * t, yl, hh),
         )
 
-    for a in range(2):
-        for t in range(2):
-            own = (c + 2 * t == x) & (hh == c)
-
-            @pl.when(jnp.logical_not(own))
-            def _():
-                s1(a, t).start()
-
-            @pl.when(own)
-            def _():
-                src, dst = ((wkv, bigk), (wqv, bigq))[a]
-                dst[z, pl.ds(pl.multiple_of(x * SLICE, SLICE), SLICE), :] = src[...]
+    def s1_sends(two_hops):
+        for a in range(2):
+            for t in range(2):
+                own = (c + 2 * t == x) & (hh == c)
+                far = home & (c + 2 * t != x)
+
+                @pl.when(far if two_hops else jnp.logical_not(own | far))
+                def _():
+                    s1(a, t).start()
+
+    s1_sends(False)
+
+    @pl.when(home & (hh == c))
+    def _():
+        for a in range(2):
+            src, dst = ((wkv, bigk), (wqv, bigq))[a]
+            dst[z, pl.ds(pl.multiple_of(x * SLICE, SLICE), SLICE), :] = src[...]
 
     send_lat = remote(lat, latb, s_l, r_l, (m, z, 2 * pair + 1 - px, yl, px))
 
@@ -154,6 +161,7 @@
     buf1[x] = shl[x]
     for j in range(1, 4):
         m1(j).wait_recv()
+    s1_sends(True)
     total = buf1[0] + buf1[1] + buf1[2] + buf1[3]
     for k in range(8):
         for j in range(2):
@@ -170,43 +178,45 @@
     def half_of(n):
         return c if n % 2 == 0 else 1 - c
 
-    def ring(a, n):
+    def piece(half, e):
+        near = jnp.where(hh == half, px, 1 - px)
+        return pl.ds((2 * half + (near if e == 0 else 1 - near)) * SLICE, SLICE)
+
+    def ring(a, n, e):
         origin = lax.rem(z - dz * (n // 2) + 8, 8)
-        spot = (bigk, bigq)[a].at[origin, pl.ds(half_of(n) * HALF, HALF), :]
-        return remote(spot, spot, s_rg.at[a, n], r_rg.at[a, n], (m, znext, x, yl, c))
-
-    def across(a, n):
+        spot = (bigk, bigq)[a].at[origin, piece(half_of(n), e), :]
+        return remote(spot, spot, s_rg.at[a, n, e], r_rg.at[a, n, e], (m, znext, x, yl, c))
+
+    def across(a, n, e):
         k = n - 1
         big = (bigk, bigq)[a]
         if n == 0:
-            spot = big.at[z, pl.ds(c * HALF, HALF), :]
+            spot = big.at[z, piece(c, e), :]
         else:
             origin = lax.rem(z - dz * (k // 2 + 1) + 8, 8)
-            spot = big.at[origin, pl.ds(half_of(k) * HALF, HALF), :]
-        return remote(spot, spot, s_dd.at[a, n], r_dd.at[a, n], sib)
-
-    def s1_arrived(a):
-        for u in range(2):
-            own = (2 * c + u == x) & home
-
-            @pl.when(jnp.logical_not(own))
-            def _():
-                src, dst = ((wkv, bigk), (wqv, bigq))[a]
-                remote(
-                    src, dst.at[z, pl.ds((2 * c + u) * SLICE, SLICE), :],
-                    s_s1.at[a, 0], r_s1.at[a, u], sib,
-                ).wait_recv()
-
-    for a in range(2):
-        s1_arrived(a)
-        ring(a, 0).start()
-        across(a, 0).start()
-
-    @pl.when(away)
-    def _():
-        send_lat.wait_recv()
-        latf[...] = jnp.zeros((8, 512), F32)
-        latf[0:3, :] = latb[...].astype(F32)
+            spot = big.at[origin, piece(half_of(k), e), :]
+        return remote(spot, spot, s_dd.at[a, n, e], r_dd.at[a, n, e], sib)
+
+    def s1_arrived(a, e):
+        near = jnp.where(hh == c, px, 1 - px)
+        u = near if e == 0 else 1 - near
+        own = (2 * c + u == x) & home
+
+        @pl.when(jnp.logical_not(own))
+        def _():
+            src, dst = ((wkv, bigk), (wqv, bigq))[a]
+            remote(
+                src, dst.at[z, pl.ds((2 * c + u) * SLICE, SLICE), :],
+                s_s1.at[a, 0], r_s1.at[a, u], sib,
+            ).wait_recv()
+
+    def set_off(e):
+        for a in range(2):
+            s1_arrived(a, e)
+            ring(a, 0, e).start()
+            across(a, 0, e).start()
+
+    set_off(0)
 
     for j in range(1, 8):
         m2(j).wait_recv()
@@ -245,9 +255,13 @@
                 at = pl.multiple_of((2 * yl + c) * 128 + k * ROW_CHUNK, ROW_CHUNK)
                 rows[pl.ds(at, ROW_CHUNK), :] = made[k * ROW_CHUNK : (k + 1) * ROW_CHUNK, :]
 
-    for a in range(2):
-        across(a, 0).wait_recv()
-        ring(a, 1).start()
+        if k == 0:
+            set_off(1)
+
+    for e in range(2):
+        for a in range(2):
+            across(a, 0, e).wait_recv()
+            ring(a, 1, e).start()
 
     def share(a, t, y2):
         h2 = 2 * y2 + t
@@ -266,22 +280,11 @@
             s_self.at[a],
         )
 
-    for t in range(2):
-        for y2 in range(2):
-            own = (2 * pair + t == x) & (y2 == yl) & home
-
-            @pl.when(jnp.logical_not(own))
-            def _():
-                share(1, t, y2).start()
-                share(0, t, y2).start()
-
-    @pl.when(home)
+    @pl.when(away)
     def _():
-        keep(0).start()
-        keep(1).start()
-
-    copy_q = remote(wqv, qo, s_q, r_q, mate)
-    copy_q.start()
+        send_lat.wait_recv()
+        latf[...] = jnp.zeros((8, 512), F32)
+        latf[0:3, :] = latb[...].astype(F32)
 
     @pl.loop(0, 4)
     def _(i):
@@ -300,13 +303,18 @@
         return remote(spot, spot, s_r2.at[p, k], r_r2.at[p, k], up if p == 0 else down)
 
     def ring_step(n):
-        for a in range(2):
-            ring(a, n).wait_recv()
-            if n + 2 < 7:
-                ring(a, n + 2).start()
-            across(a, n + 1).start()
-
-    for k in range(4):
+        for e in range(2):
+            for a in range(2):
+                ring(a, n, e).wait_recv()
+                if n + 2 < 7 and n != 4:
+                    ring(a, n + 2, e).start()
+                across(a, n + 1, e).start()
+        if n == 4:
+            for a in range(2):
+                for e in range(2):
+                    ring(a, 6, e).start()
+
+    def relay(k):
         for p in range(2):
             own = home & (c == p)
 
@@ -319,50 +327,84 @@
                 ).wait_recv()
 
             r2(p, k, yl).start()
+
+    @pl.when(home)
+    def _():
+        for k in range(4):
+            relay(k)
+
+    for k in range(4):
         ring_step(k)
 
+        @pl.when(away)
+        def _():
+            relay(k)
+
+    ring_step(4)
     for k in range(4):
         for p in range(2):
             r2(p, k, 1 - yl).wait_recv()
 
+    for t in range(2):
+        for y2 in range(2):
+            own = (2 * pair + t == x) & (y2 == yl) & home
+
+            @pl.when(jnp.logical_not(own))
+            def _():
+                share(1, t, y2).start()
+                share(0, t, y2).start()
+
+    @pl.when(home)
+    def _():
+        keep(0).start()
+        keep(1).start()
+
     def project(a, zo, first):
         acc, big = ((kacc, bigk), (qacc, bigq))[a]
         cols = pl.ds(pl.multiple_of(zo * 640, 128), 640)
 
-        @pl.loop(0, acc.shape[1] // 128)
-        def _(i):
-            lanes = pl.ds(pl.multiple_of(i * 128, 128), 128)
-            term = jnp.dot(rows[:, cols], big[zo, :, lanes], preferred_element_type=F32)
-            if first:
-                acc[:, lanes] = term
-            else:
-                acc[:, lanes] = acc[:, lanes] + term
+        term = jnp.dot(rows[:, cols], big[zo], preferred_element_type=F32)
+        acc[...] = term if first else acc[...] + term
 
     def at_distance(d):
         return lax.rem(z + d + 8, 8)
 
-    ring_step(4)
     for a in range(2):
         project(a, z, True)
     for n in range(1, 5):
         for a in range(2):
-            across(a, n).wait_recv()
-    for d in (1, -1, 2, -2):
+            for e in range(2):
+                across(a, n, e).wait_recv()
+
+    @pl.loop(0, 4)
+    def _(i):
+        d = jnp.where(i == 0, 1, jnp.where(i == 1, -1, jnp.where(i == 2, 2, -2)))
         for a in range(2):
             project(a, at_distance(d), False)
+
     ring_step(5)
     for n in (5, 6):
         for a in range(2):
-            across(a, n).wait_recv()
-    for d in (3, -3):
+            for e in range(2):
+                across(a, n, e).wait_recv()
+
+    @pl.loop(0, 2)
+    def _(i):
         for a in range(2):
-            project(a, at_distance(d), False)
+            project(a, at_distance(3 - 6 * i), False)
+
+
+    def last_in(a, e):
+        ring(a, 6, e).wait_recv()
+        across(a, 7, e).start()
 
     def last_step(a):
-        ring(a, 6).wait_recv()
-        across(a, 7).start()
-        across(a, 7).wait_recv()
+        for e in range(2):
+            across(a, 7, e).wait_recv()
         project(a, at_distance(4), False)
+
+    last_in(0, 0)
+    last_in(0, 1)
 
     def turned(pre, at):
         inverse = lax.rsqrt(jnp.mean(pre * pre, axis=1, keepdims=True) + 1e-06)
@@ -384,6 +426,8 @@
         return remote(spot, spot, s_k, r_k, mate)
 
     keys(m).start()
+    last_in(1, 0)
+    last_in(1, 1)
     last_step(1)
 
     for hd in range(4):
@@ -405,17 +449,18 @@
     scale = HEAD_SIZE ** (-0.5)
 
     def attend(first, count):
-        @pl.loop(0, 4 * count)
+        @pl.loop(0, 2 * count)
         def _(i):
-            lanes = pl.ds(pl.multiple_of((first + i // 4) * 128, 128), 128)
-            at = pl.ds(pl.multiple_of(lax.rem(i, 4) * BLOCK, BLOCK), BLOCK)
+            lanes = pl.ds(pl.multiple_of((first + i // 2) * 128, 128), 128)
+            at = pl.ds(pl.multiple_of(lax.rem(i, 2) * QUERY, QUERY), QUERY)
             inverse, normed, query = turned(qacc[at, lanes], at)
             key, value = krot[:, lanes], vals[:, lanes]
             nt = (((1,), (1,)), ((), ()))
             scores = lax.dot_general(query, key, nt, preferred_element_type=F32)
             raised = jnp.exp2(scores * (scale * math.log2(math.e)))
-            probs = raised / jnp.sum(raised, axis=1, keepdims=True)
             grad_probs = lax.dot_general(cots[at, lanes], value, nt, preferred_element_type=F32)
+            share_of = 1.0 / jnp.sum(raised, axis=1, keepdims=True)
+            probs = raised * share_of
             inner = jnp.sum(probs * grad_probs, axis=1, keepdims=True)
             grad_scores = (probs * (grad_probs - inner)).astype(BF)
             turn = jnp.dot(grad_scores, key, preferred_element_type=F32) * scale
@@ -423,129 +468,187 @@
             mean = jnp.mean(grad * normed, axis=1, keepdims=True)
             gq[at, lanes] = (inverse * (grad - normed * mean)).astype(BF)
 
+    copy_q = remote(wqv, qo, s_q, r_q, mate)
+    copy_q.start()
+
+    mine, other = pl.ds(c * HALF, HALF), pl.ds((1 - c) * HALF, HALF)
+
+    def zat(j):
+        return lax.rem(z + dz * j + 16, 8)
+
+    class Reduce:
+        def __init__(self, g, lane, bufs):
+            self.g, self.width = g, bufs[0].shape[2]
+            self.lanes = pl.ds(pl.multiple_of(lane, 128), self.width)
+            (self.own, self.sib, self.got, self.arrived, self.out, self.last, self.last_got,
+             self.last_arr, self.fin) = bufs
+
+        def squares(self, zs, dst):
+            cols = pl.ds(pl.multiple_of(zs * 640, 128), 640)
+            g = lax.dot_general(
+                rows[:, cols], gq[:, self.lanes], (((0,), (0,)), ((), ())),
+                preferred_element_type=F32,
+            )
+            dst[...] = (g * g).astype(BF)
+
+        def pass_on(self, q):
+            if q == 0:
+                src, dst = self.own.at[3, other, :], self.got.at[3, other, :]
+            elif q < 4:
+                src, dst = self.sib.at[3 - q], self.got.at[3 - q]
+            elif q == 4:
+                src, dst = self.last.at[other, :], self.last_got
+            else:
+                src, dst = self.arrived.at[5, q - 5], self.last_arr.at[q - 5]
+            return remote(src, dst, s_sd.at[self.g, q], r_sd.at[self.g, q], sib)
+
+        def passed(self, q):
+            if q == 0:
+                return remote(
+                    self.own.at[3, mine, :], self.got.at[3, mine, :],
+                    s_sd.at[self.g, q], r_sd.at[self.g, q], sib,
+                )
+            return self.pass_on(q)
+
+        def sums(self, n, u):
+            return remote(
+                self.out.at[n, u], self.arrived.at[n, u], s_sr.at[self.g, n, u],
+                r_sr.at[self.g, n, u], (m, znext, x, yl, c),
+            )
+
+        def send_on(self, n):
+            j = (8 - n) // 2 - 1
+            base = (c if n % 2 == 0 else 1 - c) * HALF
+            for u in range(2):
+                if n >= 2:
+                    self.sums(n - 2, u).wait_recv()
+
+                @pl.loop(0, SLICE // 32)
+                def _(i):
+                    at = pl.ds(pl.multiple_of(i * 32, 32), 32)
+                    far = pl.ds(pl.multiple_of(base + u * SLICE + i * 32, 32), 32)
+                    total = self.own[j, far, :].astype(F32) + self.got[j, far, :].astype(F32)
+                    if n >= 2:
+                        total = total + self.arrived[n - 2, u, at, :].astype(F32)
+                    self.out[n, u, at, :] = total.astype(BF)
+
+                self.sums(n, u).start()
+
+        def start(self):
+            self.squares(zat(4), self.own.at[3])
+            self.pass_on(0).start()
+            self.squares(zat(-3), self.sib.at[2])
+            self.pass_on(1).start()
+            self.passed(0).wait_recv()
+            self.send_on(0)
+            self.squares(zat(3), self.own.at[2])
+            self.passed(1).wait_recv()
+            self.send_on(1)
+
+        def middle(self, k):
+            self.squares(zat(k - 4), self.sib.at[3 - k])
+            self.pass_on(k).start()
+            self.squares(zat(4 - k), self.own.at[3 - k])
+            self.send_on(2 * k - 2)
+            self.passed(k).wait_recv()
+            self.send_on(2 * k - 1)
+
+        def own_slice(self):
+            self.squares(z, self.last)
+            self.pass_on(4).start()
+
+        def xs(self, u):
+            return remote(
+                self.fin.at[u], xb.at[hh, :, self.lanes], s_x.at[self.g, u], r_x.at[self.g, hh],
+                (m, z, 2 * c + u, yl, px),
+            )
+
+        def finish(self):
+            for u in range(2):
+                self.sums(5, u).wait_recv()
+                self.pass_on(5 + u).start()
+            self.passed(4).wait_recv()
+            for u in range(2):
+                self.passed(5 + u).wait_recv()
+                self.sums(6, u).wait_recv()
+
+                @pl.loop(0, SLICE // 32)
+                def _(i):
+                    at = pl.ds(pl.multiple_of(i * 32, 32), 32)
+                    near = pl.ds(pl.multiple_of(u * SLICE + i * 32, 32), 32)
+                    far = pl.ds(pl.multiple_of(c * HALF + u * SLICE + i * 32, 32), 32)
+                    total = self.last[far, :].astype(F32) + self.last_got[near, :].astype(F32)
+                    total = total + self.arrived[6, u, at, :].astype(F32)
+                    total = total + self.last_arr[u, at, :].astype(F32)
+                    self.fin[u, at, :] = total.astype(BF)
+
+                own = (2 * c + u == x) & home
+
+                @pl.when(jnp.logical_not(own))
+                def _():
+                    self.xs(u).start()
+
+                @pl.when(own)
+                def _():
+                    xb[hh, :, self.lanes] = self.fin[u]
+
+        def weigh(self):
+            for t in range(2):
+                own = (c + 2 * t == x) & (hh == c)
+
+                @pl.when(jnp.logical_not(own))
+                def _():
+                    remote(
+                        self.fin.at[0], xb.at[t, :, self.lanes], s_x.at[self.g, 0],
+                        r_x.at[self.g, t], sib,
+                    ).wait_recv()
+
+            fisher = xb[0, :, self.lanes].astype(F32) + xb[1, :, self.lanes].astype(F32)
+            wo[:, self.lanes] = (fisher + damping).astype(BF)
+            self.mate_copy().start()
+
+        def mate_copy(self):
+            return remote(
+                wo.at[:, self.lanes], wi.at[:, self.lanes], s_w.at[self.g], r_w.at[self.g], mate
+            )
+
+        def drain(self):
+            for n in range(7):
+                for u in range(2):
+                    self.sums(n, u).wait_send()
+            for q in range(7):
+                self.pass_on(q).wait_send()
+            for u in range(2):
+                own = (2 * c + u == x) & home
+
+                @pl.when(jnp.logical_not(own))
+                def _():
+                    self.xs(u).wait_send()
+
+            self.mate_copy().wait()
+
+    part_a = Reduce(0, m * 256, (own_a, sib_a, got_a, arr_a, out_a, last_a, lgot_a, larr_a, fin_a))
+    part_b = Reduce(
+        1, (1 - m) * KW, (own_b, sib_b, got_b, arr_b, out_b, last_b, lgot_b, larr_b, fin_b)
+    )
+
     attend(2 * m, 3)
+    part_a.start()
     keys(1 - m).wait_recv()
     attend(3 - 3 * m, 2)
-
-    def squares(zs, dst):
-        @pl.loop(0, 5)
-        def _(r):
-            cols = pl.ds(pl.multiple_of(zs * 640 + r * 128, 128), 128)
-            g = lax.dot_general(
-                rows[:, cols], gq[...], (((0,), (0,)), ((), ())), preferred_element_type=F32
-            )
-            dst[pl.ds(pl.multiple_of(r * 128, 128), 128), :] = (g * g).astype(BF)
-
-    mine, other = pl.ds(c * HALF, HALF), pl.ds((1 - c) * HALF, HALF)
-
-    def zat(j):
-        return lax.rem(z + dz * j + 16, 8)
-
-    def pass_on(q):
-        if q == 0:
-            src, dst = own_sq.at[3, other, :], got_sq.at[3, other, :]
-        elif q < 4:
-            src, dst = sib_sq.at[3 - q], got_sq.at[3 - q]
-        elif q == 4:
-            src, dst = last_sq.at[other, :], last_got
-        else:
-            u = q - 5
-            src, dst = arrived.at[5, u], last_arr.at[u]
-        return remote(src, dst, s_sd.at[q], r_sd.at[q], sib)
-
-    def passed(q):
-        if q == 0:
-            return remote(
-                own_sq.at[3, mine, :], got_sq.at[3, mine, :], s_sd.at[q], r_sd.at[q], sib
-            )
-        return pass_on(q)
-
-    def sums(n, u):
-        return remote(out.at[n, u], arrived.at[n, u], s_sr.at[n, u], r_sr.at[n, u], (m, znext, x, yl, c))
-
-    def send_on(n):
-        j = (8 - n) // 2 - 1
-        base = (c if n % 2 == 0 else 1 - c) * HALF
-        for u in range(2):
-            if n >= 2:
-                sums(n - 2, u).wait_recv()
-
-            @pl.loop(0, SLICE // 32)
-            def _(i):
-                at = pl.ds(pl.multiple_of(i * 32, 32), 32)
-                far = pl.ds(pl.multiple_of(base + u * SLICE + i * 32, 32), 32)
-                total = own_sq[j, far, :].astype(F32) + got_sq[j, far, :].astype(F32)
-                if n >= 2:
-                    total = total + arrived[n - 2, u, at, :].astype(F32)
-                out[n, u, at, :] = total.astype(BF)
-
-            sums(n, u).start()
-
-    squares(zat(4), own_sq.at[3])
-    pass_on(0).start()
-    squares(zat(-3), sib_sq.at[2])
-    pass_on(1).start()
-    passed(0).wait_recv()
-    send_on(0)
-    squares(zat(3), own_sq.at[2])
-    passed(1).wait_recv()
-    send_on(1)
-    squares(zat(-2), sib_sq.at[1])
-    pass_on(2).start()
-    squares(zat(2), own_sq.at[1])
-    send_on(2)
-    passed(2).wait_recv()
-    send_on(3)
-    squares(zat(-1), sib_sq.at[0])
-    pass_on(3).start()
-    squares(zat(1), own_sq.at[0])
-    send_on(4)
-    passed(3).wait_recv()
-    send_on(5)
-    squares(z, last_sq)
-    pass_on(4).start()
-    send_on(6)
-
-    def xs(u):
-        return remote(fin.at[u], xb.at[hh], s_x.at[u], r_x.at[hh], (m, z, 2 * c + u, yl, px))
-
-    for u in range(2):
-        sums(5, u).wait_recv()
-        pass_on(5 + u).start()
-    passed(4).wait_recv()
-    for u in range(2):
-        passed(5 + u).wait_recv()
-        sums(6, u).wait_recv()
-
-        @pl.loop(0, SLICE // 32)
-        def _(i):
-            at = pl.ds(pl.multiple_of(i * 32, 32), 32)
-            near = pl.ds(pl.multiple_of(u * SLICE + i * 32, 32), 32)
-            far = pl.ds(pl.multiple_of(c * HALF + u * SLICE + i * 32, 32), 32)
-            total = last_sq[far, :].astype(F32) + last_got[near, :].astype(F32)
-            total = total + arrived[6, u, at, :].astype(F32) + last_arr[u, at, :].astype(F32)
-            fin[u, at, :] = total.astype(BF)
-
-        own = (2 * c + u == x) & home
-
-        @pl.when(jnp.logical_not(own))
-        def _():
-            xs(u).start()
-
-        @pl.when(own)
-        def _():
-            xb[hh] = fin[u]
-
-    for t in range(2):
-        own = (c + 2 * t == x) & (hh == c)
-
-        @pl.when(jnp.logical_not(own))
-        def _():
-            remote(fin.at[0], xb.at[t], s_x.at[0], r_x.at[t], sib).wait_recv()
-
-    wo[...] = (xb[0].astype(F32) + xb[1].astype(F32) + damping).astype(BF)
-    copy_w = remote(wo, wi, s_w, r_w, mate)
-    copy_w.start()
+    part_a.middle(2)
+    part_b.start()
+    part_a.middle(3)
+    part_b.middle(2)
+    part_a.own_slice()
+    part_a.send_on(6)
+    part_b.middle(3)
+    part_b.own_slice()
+    part_a.finish()
+    part_b.send_on(6)
+    part_b.finish()
+    part_a.weigh()
+    part_b.weigh()
 
     for j in range(1, 4):
         m1(j).wait_send()
@@ -580,37 +683,34 @@
                 share(1, t, y2).wait_send()
 
     for a in range(2):
-        for n in range(7):
-            ring(a, n).wait_send()
-        for n in range(8):
-            across(a, n).wait_send()
+        for e in range(2):
+            for n in range(7):
+                ring(a, n, e).wait_send()
+            for n in range(8):
+                across(a, n, e).wait_send()
     for k in range(4):
         for p in range(2):
             r2(p, k, yl).wait_send()
     keys(m).wait_send()
-    for n in range(7):
-        for u in range(2):
-            sums(n, u).wait_send()
-    for q in range(7):
-        pass_on(q).wait_send()
-    for u in range(2):
-        own = (2 * c + u == x) & home
-
-        @pl.when(jnp.logical_not(own))
-        def _():
-            xs(u).wait_send()
-
     copy_q.wait()
-    copy_w.wait()
+    part_a.drain()
+    part_b.drain()
 
 
 def step(timestep, tw, lattice, tokens, own_query, own_key, values, cotangent):
     vmem = pl.BlockSpec(memory_space=pltpu.VMEM)
-    hbm = pl.BlockSpec(memory_space=pl.ANY)
+    hbm = pl.BlockSpec(memory_space=pltpu.HBM)
     dma = pltpu.SemaphoreType.DMA
 
     def v(shape, dtype=BF):
         return pltpu.VMEM(shape, dtype)
+
+    def sums_of(width):
+        return (
+            v((4, 640, width)), v((3, 640, width)), v((4, 640, width)),
+            v((7, 2, SLICE, width)), v((7, 2, SLICE, width)),
+            v((640, width)), v((HALF, width)), v((2, SLICE, width)), v((2, SLICE, width)),
+        )
 
     return pl.pallas_call(
         kernel,
@@ -630,19 +730,17 @@
             v((8, 2, 640), F32), v((8, 2, 640), F32), v((2, 5120), F32),
             v((3, 512), jnp.int32), v((8, 512), F32), v((512, 128), F32), v((512, 128), F32),
             v((512, 640), F32), v((512, KW), F32), v((512, 640)), v((512, 640)),
-            v((4, 640, 640)), v((3, 640, 640)), v((4, 640, 640)),
-            v((7, 2, SLICE, 640)), v((7, 2, SLICE, 640)),
-            v((640, 640)), v((HALF, 640)), v((2, SLICE, 640)), v((2, SLICE, 640)),
+            *sums_of(KW), *sums_of(256),
             dma((3,)), dma((2,)), dma, dma,
             dma((4,)), dma((4,)), dma((8,)), dma((8,)), dma((2, 2)), dma((2, 2)),
-            dma((2, 7)), dma((2, 7)), dma((2, 8)), dma((2, 8)),
+            dma((2, 7, 2)), dma((2, 7, 2)), dma((2, 8, 2)), dma((2, 8, 2)),
             dma((2, 4)), dma((2, 4)), dma((2, 4)), dma((2, 4)), dma((2, 2, 2)), dma((2, 4)),
             dma, dma,
-            dma((7,)), dma((7,)), dma((7, 2)), dma((7, 2)), dma((2,)), dma((2,)),
-            dma, dma, dma, dma,
+            dma((2, 7)), dma((2, 7)), dma((2, 7, 2)), dma((2, 7, 2)), dma((2, 2)), dma((2, 2)),
+            dma, dma, dma((2,)), dma((2,)),
         ],
         compiler_params=pltpu.CompilerParams(
-            collective_id=0, has_side_effects=True, vmem_limit_bytes=60 * 1024 * 1024
+            collective_id=0, has_side_effects=True, vmem_limit_bytes=58 * 1024 * 1024
         ),
         name="fisher_step",
     )(timestep, tw, lattice, tokens, own_query, own_key, values, cotangent)

time: 173 us -> 138 us (0.80)
  the two profiles are of different devices: /device:TPU:1 before, /device:TPU:32 now
where the time goes in v3:
time: 138 us
  Pallas kernels  133 us (96%)
  other arithmetic  4 us (3%)
    pallas_call x1, Pallas kernels, step(): pl.pallas_call(kernel, out_shape=(jax.ShapeDtypeStruct((2, SLICE, 640), B...  133 us

profile of v3, /device:TPU:32, one launch (start us, length us, event | category | flops | bytes accessed | tf_op | source)
XLA Modules:
  0.0 138.0 jit_solution(13810354533823878557)
XLA Ops:
  0.6 133.4 %fisher_step.1 = (bf16[2,160,640]{2,1,0:T(8,128)(2,1)}, bf16[160,640]{1,0:T(8,128)(2,1)}, bf16[160,640]{1,0:T(8,128)(2,1)}, bf16[160,640]{1,0:T(8,128)(2,1)}, bf16[160,640]{1,0:T(8,128)(2,1)}) custom-call(s32[32]{0:T(128)} %when.1, bf16[2,160,256]{2,1,0:T(8,128)(2,1)} %bitcast.5, s32[3,512]{1,0:T(4,128)} %lat.1, bf16[128,5120]{1,0:T(8,128)(2,1)} %tok_hbm.1, ...), custom_call_target="tpu_custom_call" | custom-call | tf_op jit(solution)/shard_map/fisher_step/pallas_call | solution.py:715
  134.0 1.8 %convert_add_fusion.1 = f32[1,160,640]{2,1,0:T(8,128)} fusion(bf16[2,160,640]{2,1,0:T(8,128)(2,1)} %get-tuple-element.7), kind=kLoop, calls=%fused_computation.5 | loop fusion | flops 307200 | bytes 819200 | tf_op jit(solution)/shard_map/add | solution.py:755
  135.9 2.2 %fusion.1 = f32[160,640]{1,0:T(8,128)} fusion(bf16[160,640]{1,0:T(8,128)(2,1)} %get-tuple-element.11, bf16[160,640]{1,0:T(8,128)(2,1)} %get-tuple-element.10, bf16[160,640]{1,0:T(8,128)(2,1)} %get-tuple-element.9, bf16[160,640]{1,0:T(8,128)(2,1)} %get-tuple-element.8, pred[]{:T(512)S(6)} %eq.3), kind=kLoop, calls=%fused_computation.4 | loop fusion | flops 1331200 | bytes 1228801 | tf_op jit(solution)/shard_map/div | solution.py:759

commit v4 on v3

--- a/solution.py
+++ b/solution.py
@@ -54,10 +54,10 @@
 
 
 def kernel(
-    when, tw, lat, tok_hbm, wq_hbm, wk_hbm, val, cot,
+    when, tw_hbm, lat_hbm, tok_hbm, wq_hbm, wk_hbm, val, cot,
     xb, wo, wi, qo, wqv,
     tok, wkv, bigq, bigk, rows, vals, cots, made,
-    ang, wide, shl, buf1, tot, buf2, mod, latb, latf, cosb, sinb,
+    tw, lat, ang, wide, shl, buf1, tot, buf2, mod, latb, latf, cosb, sinb,
     qacc, kacc, krot, gq,
     own_a, sib_a, got_a, arr_a, out_a, last_a, lgot_a, larr_a, fin_a,
     own_b, sib_b, got_b, arr_b, out_b, last_b, lgot_b, larr_b, fin_b,
@@ -81,9 +81,23 @@
         pltpu.make_async_copy(wk_hbm.at[:, pl.ds(pl.multiple_of(m * 256, 128), KW)], wkv, s_in.at[0]),
         pltpu.make_async_copy(wq_hbm, wqv, s_in.at[1]),
         pltpu.make_async_copy(tok_hbm, tok, s_in.at[2]),
+        pltpu.make_async_copy(tw_hbm, tw, s_in.at[5]),
+        pltpu.make_async_copy(lat_hbm, lat, s_in.at[6]),
     ]
     for load in loads:
         load.start()
+    key_columns = pl.ds(pl.multiple_of(m * 256, 128), KW)
+    own_weights = [
+        pltpu.make_async_copy(
+            wk_hbm.at[:, key_columns], bigk.at[z, pl.ds(x * SLICE, SLICE), :], s_in.at[3]
+        ),
+        pltpu.make_async_copy(wq_hbm, bigq.at[z, pl.ds(x * SLICE, SLICE), :], s_in.at[4]),
+    ]
+
+    @pl.when(home)
+    def _():
+        for load in own_weights:
+            load.start()
 
     for j in range(1, 16):
         q = lax.rem(x * 4 + yl * 2 + c + j, 16)
@@ -99,6 +113,8 @@
         for b in range(8):
             r = a * 8 + b
             ang[r : r + 1, :] = when[b * 4 + a].astype(F32) * frequency
+    loads[3].wait()
+    loads[4].wait()
     for j in range(2):
         wide[j] = jnp.zeros((640, 256), BF)
         wide[j, pl.ds(pl.multiple_of(x * SLICE, SLICE), SLICE), :] = tw[j]
@@ -141,42 +157,13 @@
 
     s1_sends(False)
 
-    @pl.when(home & (hh == c))
-    def _():
-        for a in range(2):
-            src, dst = ((wkv, bigk), (wqv, bigq))[a]
-            dst[z, pl.ds(pl.multiple_of(x * SLICE, SLICE), SLICE), :] = src[...]
-
-    send_lat = remote(lat, latb, s_l, r_l, (m, z, 2 * pair + 1 - px, yl, px))
-
     @pl.when(home)
     def _():
-        latf[...] = jnp.zeros((8, 512), F32)
-        latf[0:3, :] = lat[...].astype(F32)
-
-    @pl.when(home)
-    def _():
-        send_lat.start()
-
-    buf1[x] = shl[x]
-    for j in range(1, 4):
-        m1(j).wait_recv()
-    s1_sends(True)
-    total = buf1[0] + buf1[1] + buf1[2] + buf1[3]
-    for k in range(8):
-        for j in range(2):
-            tot[k, j : j + 1, :] = total[j, k : k + 1, :]
-
-    def m2(j):
-        to = lax.rem(z + j, 8)
-        return remote(tot.at[to], buf2.at[z], s_m2.at[j], r_m2.at[j], (m, to, x, yl, c))
-
-    for j in range(1, 8):
-        m2(j).start()
-    buf2[z] = tot[z]
+        for load in own_weights:
+            load.wait()
 
     def half_of(n):
-        return c if n % 2 == 0 else 1 - c
+        return c if n == 6 else (hh if n % 2 == 0 else 1 - hh)
 
     def piece(half, e):
         near = jnp.where(hh == half, px, 1 - px)
@@ -210,13 +197,103 @@
                 s_s1.at[a, 0], r_s1.at[a, u], sib,
             ).wait_recv()
 
-    def set_off(e):
-        for a in range(2):
-            s1_arrived(a, e)
-            ring(a, 0, e).start()
-            across(a, 0, e).start()
-
-    set_off(0)
+    collector = hh == c
+
+    def set_off(n, e):
+        gathers = collector if n == 0 else jnp.logical_not(collector)
+
+        @pl.when(gathers)
+        def _():
+            for a in range(2):
+                s1_arrived(a, e)
+                ring(a, n, e).start()
+                if (n, e) == (0, 0):
+
+                    @pl.when(home)
+                    def _():
+                        across(a, 0, e).start()
+                else:
+                    across(a, 0, e).start()
+
+        @pl.when(jnp.logical_not(gathers))
+        def _():
+            for a in range(2):
+                if (n, e) == (0, 0):
+
+                    @pl.when(away)
+                    def _():
+                        across(a, 0, e).wait_recv()
+                else:
+                    across(a, 0, e).wait_recv()
+                ring(a, n, e).start()
+
+    def share(a, t, y2):
+        h2 = 2 * y2 + t
+        src, dst = ((val, vals), (cot, cots))[a]
+        return remote(
+            src.at[:, h2 * 640 : (h2 + 1) * 640],
+            dst.at[pl.ds((2 * yl + c) * 128, 128), :],
+            s_v.at[a, t, y2], r_v.at[a, 2 * yl + c], (m, z, 2 * pair + t, y2, px),
+        )
+
+    def keep(a):
+        src, dst = ((val, vals), (cot, cots))[a]
+        return pltpu.make_async_copy(
+            src.at[:, pl.ds(pl.multiple_of((2 * yl + px) * 640, 128), 640)],
+            dst.at[pl.ds((2 * yl + c) * 128, 128), :],
+            s_self.at[a],
+        )
+
+    def shares(x_moves, y_moves):
+        for t in range(2):
+            for y2 in range(2):
+                own = (2 * pair + t == x) & (y2 == yl) & home
+                kind = ((2 * pair + t != x) == x_moves) & ((y2 != yl) == y_moves)
+
+                @pl.when(kind & jnp.logical_not(own))
+                def _():
+                    share(1, t, y2).start()
+                    share(0, t, y2).start()
+
+    set_off(0, 0)
+    shares(False, True)
+    shares(False, False)
+
+    @pl.when(home)
+    def _():
+        keep(0).start()
+        keep(1).start()
+
+
+    send_lat = remote(lat, latb, s_l, r_l, (m, z, 2 * pair + 1 - px, yl, px))
+
+    @pl.when(home)
+    def _():
+        latf[...] = jnp.zeros((8, 512), F32)
+        latf[0:3, :] = lat[...].astype(F32)
+
+    @pl.when(home)
+    def _():
+        send_lat.start()
+
+    buf1[x] = shl[x]
+    for j in range(1, 4):
+        m1(j).wait_recv()
+    total = buf1[0] + buf1[1] + buf1[2] + buf1[3]
+    for k in range(8):
+        for j in range(2):
+            tot[k, j : j + 1, :] = total[j, k : k + 1, :]
+
+    def m2(j):
+        to = lax.rem(z + j, 8)
+        return remote(tot.at[to], buf2.at[z], s_m2.at[j], r_m2.at[j], (m, to, x, yl, c))
+
+    for j in range(1, 8):
+        m2(j).start()
+    buf2[z] = tot[z]
+
+    set_off(0, 1)
+    s1_sends(True)
 
     for j in range(1, 8):
         m2(j).wait_recv()
@@ -255,30 +332,33 @@
                 at = pl.multiple_of((2 * yl + c) * 128 + k * ROW_CHUNK, ROW_CHUNK)
                 rows[pl.ds(at, ROW_CHUNK), :] = made[k * ROW_CHUNK : (k + 1) * ROW_CHUNK, :]
 
-        if k == 0:
-            set_off(1)
-
-    for e in range(2):
-        for a in range(2):
-            across(a, 0, e).wait_recv()
-            ring(a, 1, e).start()
-
-    def share(a, t, y2):
-        h2 = 2 * y2 + t
-        src, dst = ((val, vals), (cot, cots))[a]
-        return remote(
-            src.at[:, h2 * 640 : (h2 + 1) * 640],
-            dst.at[pl.ds((2 * yl + c) * 128, 128), :],
-            s_v.at[a, t, y2], r_v.at[a, 2 * yl + c], (m, z, 2 * pair + t, y2, px),
-        )
-
-    def keep(a):
-        src, dst = ((val, vals), (cot, cots))[a]
-        return pltpu.make_async_copy(
-            src.at[:, pl.ds(pl.multiple_of((2 * yl + px) * 640, 128), 640)],
-            dst.at[pl.ds((2 * yl + c) * 128, 128), :],
-            s_self.at[a],
-        )
+    def r2(p, k, ylo):
+        spot = rows.at[pl.ds((2 * ylo + p) * 128 + k * ROW_CHUNK, ROW_CHUNK), :]
+        return remote(spot, spot, s_r2.at[p, k], r_r2.at[p, k], up if p == 0 else down)
+
+    def relay(k):
+        for p in range(2):
+            own = home & (c == p)
+
+            @pl.when(jnp.logical_not(own))
+            def _():
+                spot = rows.at[pl.ds((2 * yl + p) * 128 + k * ROW_CHUNK, ROW_CHUNK), :]
+                remote(
+                    made.at[pl.ds(k * ROW_CHUNK, ROW_CHUNK), :],
+                    spot, s_r1.at[0, k], r_r1.at[p, k], sib,
+                ).wait_recv()
+
+            r2(p, k, yl).start()
+
+    @pl.when(home)
+    def _():
+        for k in range(4):
+            relay(k)
+
+    set_off(1, 0)
+    set_off(1, 1)
+    shares(True, False)
+
 
     @pl.when(away)
     def _():
@@ -298,95 +378,66 @@
         sine = jnp.sin(angles)
         sinb[pl.ds(at, BLOCK), :] = jnp.where(column < HEAD_SIZE // 2, -sine, sine)
 
-    def r2(p, k, ylo):
-        spot = rows.at[pl.ds((2 * ylo + p) * 128 + k * ROW_CHUNK, ROW_CHUNK), :]
-        return remote(spot, spot, s_r2.at[p, k], r_r2.at[p, k], up if p == 0 else down)
-
     def ring_step(n):
         for e in range(2):
             for a in range(2):
                 ring(a, n, e).wait_recv()
-                if n + 2 < 7 and n != 4:
+                if n < 4:
                     ring(a, n + 2, e).start()
                 across(a, n + 1, e).start()
-        if n == 4:
-            for a in range(2):
-                for e in range(2):
-                    ring(a, 6, e).start()
-
-    def relay(k):
-        for p in range(2):
-            own = home & (c == p)
-
-            @pl.when(jnp.logical_not(own))
+        if n >= 4:
+
+            @pl.when(collector if n == 4 else jnp.logical_not(collector))
             def _():
-                spot = rows.at[pl.ds((2 * yl + p) * 128 + k * ROW_CHUNK, ROW_CHUNK), :]
-                remote(
-                    made.at[pl.ds(k * ROW_CHUNK, ROW_CHUNK), :],
-                    spot, s_r1.at[0, k], r_r1.at[p, k], sib,
-                ).wait_recv()
-
-            r2(p, k, yl).start()
-
-    @pl.when(home)
-    def _():
-        for k in range(4):
-            relay(k)
-
+                for a in range(2):
+                    for e in range(2):
+                        ring(a, 6, e).start()
+
+    ring_step(0)
     for k in range(4):
-        ring_step(k)
+        ring_step(k + 1)
 
         @pl.when(away)
         def _():
             relay(k)
 
-    ring_step(4)
+    def project(a, zo, first, part=None):
+        acc, big = ((kacc, bigk), (qacc, bigq))[a]
+        cols = pl.ds(pl.multiple_of(zo * 640, 128), 640)
+
+        at = slice(None) if part is None else pl.ds(pl.multiple_of(part * 256, 256), 256)
+        term = jnp.dot(rows[at, cols], big[zo], preferred_element_type=F32)
+        acc[at, :] = term if first else acc[at, :] + term
+
+    def at_distance(d):
+        return lax.rem(z + d + 8, 8)
+
+    def near_slices(part):
+        for a in range(2):
+            project(a, z, True, part)
+
+        @pl.loop(0, 4)
+        def _(i):
+            d = jnp.where(i == 0, 1, jnp.where(i == 1, -1, jnp.where(i == 2, 2, -2)))
+            for a in range(2):
+                project(a, at_distance(d), False, part)
+
+    def crossed(*steps):
+        for n in steps:
+            for a in range(2):
+                for e in range(2):
+                    across(a, n, e).wait_recv()
+
+    crossed(1, 2, 3, 4)
+    near_slices(yl)
+    ring_step(5)
     for k in range(4):
         for p in range(2):
             r2(p, k, 1 - yl).wait_recv()
 
-    for t in range(2):
-        for y2 in range(2):
-            own = (2 * pair + t == x) & (y2 == yl) & home
-
-            @pl.when(jnp.logical_not(own))
-            def _():
-                share(1, t, y2).start()
-                share(0, t, y2).start()
-
-    @pl.when(home)
-    def _():
-        keep(0).start()
-        keep(1).start()
-
-    def project(a, zo, first):
-        acc, big = ((kacc, bigk), (qacc, bigq))[a]
-        cols = pl.ds(pl.multiple_of(zo * 640, 128), 640)
-
-        term = jnp.dot(rows[:, cols], big[zo], preferred_element_type=F32)
-        acc[...] = term if first else acc[...] + term
-
-    def at_distance(d):
-        return lax.rem(z + d + 8, 8)
-
-    for a in range(2):
-        project(a, z, True)
-    for n in range(1, 5):
-        for a in range(2):
-            for e in range(2):
-                across(a, n, e).wait_recv()
-
-    @pl.loop(0, 4)
-    def _(i):
-        d = jnp.where(i == 0, 1, jnp.where(i == 1, -1, jnp.where(i == 2, 2, -2)))
-        for a in range(2):
-            project(a, at_distance(d), False)
-
-    ring_step(5)
-    for n in (5, 6):
-        for a in range(2):
-            for e in range(2):
-                across(a, n, e).wait_recv()
+    shares(True, True)
+    near_slices(1 - yl)
+    crossed(5, 6)
 
     @pl.loop(0, 2)
     def _(i):
@@ -448,25 +499,28 @@
 
     scale = HEAD_SIZE ** (-0.5)
 
+    def one_block(lanes, at):
+        inverse, normed, query = turned(qacc[at, lanes], at)
+        key, value = krot[:, lanes], vals[:, lanes]
+        nt = (((1,), (1,)), ((), ()))
+        scores = lax.dot_general(query, key, nt, preferred_element_type=F32)
+        raised = jnp.exp2(scores * (scale * math.log2(math.e)))
+        grad_probs = lax.dot_general(cots[at, lanes], value, nt, preferred_element_type=F32)
+        share_of = 1.0 / jnp.sum(raised, axis=1, keepdims=True)
+        probs = raised * share_of
+        inner = jnp.sum(probs * grad_probs, axis=1, keepdims=True)
+        grad_scores = (probs * (grad_probs - inner)).astype(BF)
+        turn = jnp.dot(grad_scores, key, preferred_element_type=F32) * scale
+        grad = turn * cosb[at, :] + pltpu.roll(turn * sinb[at, :], HEAD_SIZE // 2, 1)
+        mean = jnp.mean(grad * normed, axis=1, keepdims=True)
+        gq[at, lanes] = (inverse * (grad - normed * mean)).astype(BF)
+
     def attend(first, count):
-        @pl.loop(0, 2 * count)
+        @pl.loop(0, count)
         def _(i):
-            lanes = pl.ds(pl.multiple_of((first + i // 2) * 128, 128), 128)
-            at = pl.ds(pl.multiple_of(lax.rem(i, 2) * QUERY, QUERY), QUERY)
-            inverse, normed, query = turned(qacc[at, lanes], at)
-            key, value = krot[:, lanes], vals[:, lanes]
-            nt = (((1,), (1,)), ((), ()))
-            scores = lax.dot_general(query, key, nt, preferred_element_type=F32)
-            raised = jnp.exp2(scores * (scale * math.log2(math.e)))
-            grad_probs = lax.dot_general(cots[at, lanes], value, nt, preferred_element_type=F32)
-            share_of = 1.0 / jnp.sum(raised, axis=1, keepdims=True)
-            probs = raised * share_of
-            inner = jnp.sum(probs * grad_probs, axis=1, keepdims=True)
-            grad_scores = (probs * (grad_probs - inner)).astype(BF)
-            turn = jnp.dot(grad_scores, key, preferred_element_type=F32) * scale
-            grad = turn * cosb[at, :] + pltpu.roll(turn * sinb[at, :], HEAD_SIZE // 2, 1)
-            mean = jnp.mean(grad * normed, axis=1, keepdims=True)
-            gq[at, lanes] = (inverse * (grad - normed * mean)).astype(BF)
+            lanes = pl.ds(pl.multiple_of((first + i) * 128, 128), 128)
+            for b in range(512 // QUERY):
+                one_block(lanes, pl.ds(b * QUERY, QUERY))
 
     copy_q = remote(wqv, qo, s_q, r_q, mate)
     copy_q.start()
@@ -686,8 +740,13 @@
         for e in range(2):
             for n in range(7):
                 ring(a, n, e).wait_send()
-            for n in range(8):
+            for n in range(1, 8):
                 across(a, n, e).wait_send()
+        across(a, 0, 1).wait_send()
+
+        @pl.when(jnp.logical_not(collector & away))
+        def _():
+            across(a, 0, 0).wait_send()
     for k in range(4):
         for p in range(2):
             r2(p, k, yl).wait_send()
@@ -704,6 +763,9 @@
 
     def v(shape, dtype=BF):
         return pltpu.VMEM(shape, dtype)
+
+    def in_hbm(a):
+        return pltpu.with_memory_space_constraint(a, pltpu.HBM)
 
     def sums_of(width):
         return (
@@ -721,17 +783,17 @@
             jax.ShapeDtypeStruct((SLICE, 640), BF),
             jax.ShapeDtypeStruct((SLICE, 640), BF),
         ),
-        in_specs=[pl.BlockSpec(memory_space=pltpu.SMEM), vmem, vmem] + [hbm] * 5,
+        in_specs=[pl.BlockSpec(memory_space=pltpu.SMEM)] + [hbm] * 7,
         out_specs=(vmem,) * 5,
         scratch_shapes=[
             v((128, 5120)), v((SLICE, KW)), v((8, 640, 640)), v((8, 640, KW)),
             v((512, 5120)), v((512, 640)), v((512, 640)), v((128, 5120)),
-            v((32, 128), F32), v((2, 640, 256)), v((4, 2, 8, 640), F32), v((4, 2, 8, 640), F32),
+            v((2, SLICE, 256)), v((3, 512), jnp.int32), v((32, 128), F32), v((2, 640, 256)), v((4, 2, 8, 640), F32), v((4, 2, 8, 640), F32),
             v((8, 2, 640), F32), v((8, 2, 640), F32), v((2, 5120), F32),
             v((3, 512), jnp.int32), v((8, 512), F32), v((512, 128), F32), v((512, 128), F32),
             v((512, 640), F32), v((512, KW), F32), v((512, 640)), v((512, 640)),
             *sums_of(KW), *sums_of(256),
-            dma((3,)), dma((2,)), dma, dma,
+            dma((7,)), dma((2,)), dma, dma,
             dma((4,)), dma((4,)), dma((8,)), dma((8,)), dma((2, 2)), dma((2, 2)),
             dma((2, 7, 2)), dma((2, 7, 2)), dma((2, 8, 2)), dma((2, 8, 2)),
             dma((2, 4)), dma((2, 4)), dma((2, 4)), dma((2, 4)), dma((2, 2, 2)), dma((2, 4)),
@@ -740,10 +802,10 @@
             dma, dma, dma((2,)), dma((2,)),
         ],
         compiler_params=pltpu.CompilerParams(
-            collective_id=0, has_side_effects=True, vmem_limit_bytes=58 * 1024 * 1024
+            collective_id=0, has_side_effects=True, vmem_limit_bytes=52 * 1024 * 1024
         ),
         name="fisher_step",
-    )(timestep, tw, lattice, tokens, own_query, own_key, values, cotangent)
+    )(timestep, *(in_hbm(a) for a in (tw, lattice, tokens, own_query, own_key, values, cotangent)))
 
 
 def on_device(tokens, lattice, timestep, time_weight, query_weight, key_weight, values, cotangent):

time: 138 us -> 127 us (0.920)
  the two profiles are of different devices: /device:TPU:32 before, /device:TPU:1 now
where the time goes in v4:
time: 127 us; the launch traced here: 126 us
  Pallas kernels  123 us (97%)
  other arithmetic  1.74 us (1%)
    pallas_call x1, Pallas kernels, step(): pl.pallas_call(kernel, out_shape=(jax.ShapeDtypeStruct((2, SLICE, 640), B...  123 us

profile of v4, /device:TPU:1, one launch (start us, length us, event | category | flops | bytes accessed | tf_op | source)
XLA Modules:
  0.0 125.7 jit_solution(7528299481856956486)
XLA Ops:
  0.6 0.0 copy-start
  0.6 0.6 copy-done
  1.3 122.7 %fisher_step.1 = (bf16[2,160,640]{2,1,0:T(8,128)(2,1)S(1)}, bf16[160,640]{1,0:T(8,128)(2,1)S(1)}, bf16[160,640]{1,0:T(8,128)(2,1)S(1)}, bf16[160,640]{1,0:T(8,128)(2,1)S(1)}, bf16[160,640]{1,0:T(8,128)(2,1)S(1)}) custom-call(s32[32]{0:T(128)S(1)} %copy-done, bf16[2,160,256]{2,1,0:T(8,128)(2,1)} %bitcast.5, s32[3,512]{1,0:T(4,128)} %lat_hbm.1, ...), custom_call_target="tpu_custom_call" | custom-call | tf_op jit(solution)/shard_map/fisher_step/pallas_call | solution.py:777
  124.0 0.8 convert_add_fusion.1
  124.8 0.9 fusion.1
Async XLA Ops:
  0.6 0.7 copy-start

commit v5 on v4

--- a/solution.py
+++ b/solution.py
@@ -55,8 +55,8 @@
 
 def kernel(
     when, tw_hbm, lat_hbm, tok_hbm, wq_hbm, wk_hbm, val, cot,
-    xb, wo, wi, qo, wqv,
-    tok, wkv, bigq, bigk, rows, vals, cots, made,
+    xb, wi, qo, wqv,
+    wo, tok, wkv, bigq, bigk, rows, vals, cots, made,
     tw, lat, ang, wide, shl, buf1, tot, buf2, mod, latb, latf, cosb, sinb,
     qacc, kacc, krot, gq,
     own_a, sib_a, got_a, arr_a, out_a, last_a, lgot_a, larr_a, fin_a,
@@ -131,9 +131,13 @@
 
     pl.semaphore_wait(pltpu.get_barrier_semaphore(), 24)
 
+    window = pl.ds(pl.multiple_of(x * 128, 128), 256)
+
     def m1(j):
         to = lax.rem(x + j, 4)
-        return remote(shl.at[to], buf1.at[x], s_m1.at[j], r_m1.at[j], (m, z, to, yl, c))
+        return remote(
+            shl.at[to, :, :, window], buf1.at[x], s_m1.at[j], r_m1.at[j], (m, z, to, yl, c)
+        )
 
     for j in range(1, 4):
         m1(j).start()
@@ -276,13 +280,16 @@
     def _():
         send_lat.start()
 
-    buf1[x] = shl[x]
+    buf1[x] = shl[x, :, :, window]
     for j in range(1, 4):
         m1(j).wait_recv()
-    total = buf1[0] + buf1[1] + buf1[2] + buf1[3]
-    for k in range(8):
-        for j in range(2):
-            tot[k, j : j + 1, :] = total[j, k : k + 1, :]
+    for j in range(2):
+        lower = [buf1[a, j, :, 0:128] for a in range(4)]
+        upper = [buf1[a, j, :, 128:256] for a in range(4)]
+        tiles = [lower[0], *(upper[a] + lower[a + 1] for a in range(3)), upper[3]]
+        total = jnp.concatenate(tiles, axis=1)
+        for k in range(8):
+            tot[k, j : j + 1, :] = total[k : k + 1, :]
 
     def m2(j):
         to = lax.rem(z + j, 8)
@@ -294,6 +301,7 @@
 
     set_off(0, 1)
     s1_sends(True)
+    set_off(1, 0)
 
     for j in range(1, 8):
         m2(j).wait_recv()
@@ -355,7 +363,6 @@
         for k in range(4):
             relay(k)
 
-    set_off(1, 0)
     set_off(1, 1)
     shares(True, False)
 
@@ -781,14 +788,13 @@
             jax.ShapeDtypeStruct((SLICE, 640), BF),
             jax.ShapeDtypeStruct((SLICE, 640), BF),
             jax.ShapeDtypeStruct((SLICE, 640), BF),
-            jax.ShapeDtypeStruct((SLICE, 640), BF),
         ),
         in_specs=[pl.BlockSpec(memory_space=pltpu.SMEM)] + [hbm] * 7,
-        out_specs=(vmem,) * 5,
+        out_specs=(vmem,) * 4,
         scratch_shapes=[
-            v((128, 5120)), v((SLICE, KW)), v((8, 640, 640)), v((8, 640, KW)),
+            v((SLICE, 640)), v((128, 5120)), v((SLICE, KW)), v((8, 640, 640)), v((8, 640, KW)),
             v((512, 5120)), v((512, 640)), v((512, 640)), v((128, 5120)),
-            v((2, SLICE, 256)), v((3, 512), jnp.int32), v((32, 128), F32), v((2, 640, 256)), v((4, 2, 8, 640), F32), v((4, 2, 8, 640), F32),
+            v((2, SLICE, 256)), v((3, 512), jnp.int32), v((32, 128), F32), v((2, 640, 256)), v((4, 2, 8, 640), F32), v((4, 2, 8, 256), F32),
             v((8, 2, 640), F32), v((8, 2, 640), F32), v((2, 5120), F32),
             v((3, 512), jnp.int32), v((8, 512), F32), v((512, 128), F32), v((512, 128), F32),
             v((512, 640), F32), v((512, KW), F32), v((512, 640)), v((512, 640)),
@@ -805,18 +811,19 @@
             collective_id=0, has_side_effects=True, vmem_limit_bytes=52 * 1024 * 1024
         ),
         name="fisher_step",
-    )(timestep, *(in_hbm(a) for a in (tw, lattice, tokens, own_query, own_key, values, cotangent)))
+    )(in_hbm(timestep), *(in_hbm(a) for a in (tw, lattice, tokens, own_query, own_key, values, cotangent)))
 
 
 def on_device(tokens, lattice, timestep, time_weight, query_weight, key_weight, values, cotangent):
     member = lax.axis_index("member")
-    xb, wo, wi, qo, mine = step(
+    xb, other, qo, mine = step(
         timestep, time_weight.transpose(0, 2, 1), lattice, tokens,
         query_weight[0], key_weight, values, cotangent[0],
     )
     fisher = xb[0].astype(F32) + xb[1].astype(F32)
     first = member == 0
-    w0, w1 = jnp.where(first, wo, wi).astype(F32), jnp.where(first, wi, wo).astype(F32)
+    own, other = lax.reduce_precision(fisher + damping, 8, 7), other.astype(F32)
+    w0, w1 = jnp.where(first, own, other), jnp.where(first, other, own)
     q0, q1 = jnp.where(first, mine, qo).astype(F32), jnp.where(first, qo, mine).astype(F32)
     return (fisher[None], (w0 * q0 + w1 * q1) / (w0 + w1))
 

time: 127 us -> 124 us (0.976)
  no operation moved by 1% of the time
where the time goes in v5:
time: 124 us
  Pallas kernels  122 us (98%)
    pallas_call x1, Pallas kernels, step(): pl.pallas_call(kernel, out_shape=(jax.ShapeDtypeStruct((2, SLICE, 640), B...  122 us

profile of v5, /device:TPU:1, one launch (start us, length us, event | category | flops | bytes accessed | tf_op | source)
XLA Modules:
  0.0 123.9 jit_solution(13589686257236152639)
XLA Ops:
  0.6 122.1 %fisher_step.1 = (bf16[2,160,640]{2,1,0:T(8,128)(2,1)S(1)}, bf16[160,640]{1,0:T(8,128)(2,1)S(1)}, bf16[160,640]{1,0:T(8,128)(2,1)S(1)}, bf16[160,640]{1,0:T(8,128)(2,1)S(1)}) custom-call(s32[32]{0:T(128)} %when.1, bf16[2,160,256]{2,1,0:T(8,128)(2,1)} %bitcast.12, s32[3,512]{1,0:T(4,128)} %lat_hbm.1, bf16[128,5120]{1,0:T(8,128)(2,1)} %tok_hbm.1, ...), custom_call_target="tpu_custom_call" | custom-call | tf_op jit(solution)/shard_map/fisher_step/pallas_call | solution.py:784
  122.8 1.1 add_divide_fusion

commit v6 on v5

--- a/solution.py
+++ b/solution.py
@@ -56,7 +56,7 @@
 def kernel(
     when, tw_hbm, lat_hbm, tok_hbm, wq_hbm, wk_hbm, val, cot,
     xb, wi, qo, wqv,
-    wo, tok, wkv, bigq, bigk, rows, vals, cots, made,
+    wo, tok, wkv, bigq, bigqb, bigk, rows, vals, cots, made,
     tw, lat, ang, wide, shl, buf1, tot, buf2, mod, latb, latf, cosb, sinb,
     qacc, kacc, krot, gq,
     own_a, sib_a, got_a, arr_a, out_a, last_a, lgot_a, larr_a, fin_a,
@@ -86,12 +86,23 @@
     ]
     for load in loads:
         load.start()
-    key_columns = pl.ds(pl.multiple_of(m * 256, 128), KW)
+    lanes_a = pl.ds(pl.multiple_of(m * 256, 128), KW)
+    lanes_b = pl.ds(pl.multiple_of((1 - m) * KW, 128), 256)
+    gathered = (bigk, bigq, bigqb)
+
+    def weights_of(a):
+        return (wkv, wqv.at[:, lanes_a], wqv.at[:, lanes_b])[a]
+
     own_weights = [
         pltpu.make_async_copy(
-            wk_hbm.at[:, key_columns], bigk.at[z, pl.ds(x * SLICE, SLICE), :], s_in.at[3]
+            wk_hbm.at[:, lanes_a], bigk.at[z, pl.ds(x * SLICE, SLICE), :], s_in.at[3]
         ),
-        pltpu.make_async_copy(wq_hbm, bigq.at[z, pl.ds(x * SLICE, SLICE), :], s_in.at[4]),
+        pltpu.make_async_copy(
+            wq_hbm.at[:, lanes_a], bigq.at[z, pl.ds(x * SLICE, SLICE), :], s_in.at[4]
+        ),
+        pltpu.make_async_copy(
+            wq_hbm.at[:, lanes_b], bigqb.at[z, pl.ds(x * SLICE, SLICE), :], s_in.at[7]
+        ),
     ]
 
     @pl.when(home)
@@ -143,14 +154,14 @@
         m1(j).start()
 
     def s1(a, t):
-        src, dst = ((wkv, bigk), (wqv, bigq))[a]
+        src, dst = weights_of(a), gathered[a]
         return remote(
             src, dst.at[z, pl.ds(x * SLICE, SLICE), :], s_s1.at[a, t],
             r_s1.at[a, lax.rem(x, 2)], (m, z, c + 2 * t, yl, hh),
         )
 
-    def s1_sends(two_hops):
-        for a in range(2):
+    def s1_sends(two_hops, arrays=(0, 1)):
+        for a in arrays:
             for t in range(2):
                 own = (c + 2 * t == x) & (hh == c)
                 far = home & (c + 2 * t != x)
@@ -175,12 +186,12 @@
 
     def ring(a, n, e):
         origin = lax.rem(z - dz * (n // 2) + 8, 8)
-        spot = (bigk, bigq)[a].at[origin, piece(half_of(n), e), :]
+        spot = gathered[a].at[origin, piece(half_of(n), e), :]
         return remote(spot, spot, s_rg.at[a, n, e], r_rg.at[a, n, e], (m, znext, x, yl, c))
 
     def across(a, n, e):
         k = n - 1
-        big = (bigk, bigq)[a]
+        big = gathered[a]
         if n == 0:
             spot = big.at[z, piece(c, e), :]
         else:
@@ -195,7 +206,7 @@
 
         @pl.when(jnp.logical_not(own))
         def _():
-            src, dst = ((wkv, bigk), (wqv, bigq))[a]
+            src, dst = weights_of(a), gathered[a]
             remote(
                 src, dst.at[z, pl.ds((2 * c + u) * SLICE, SLICE), :],
                 s_s1.at[a, 0], r_s1.at[a, u], sib,
@@ -203,12 +214,12 @@
 
     collector = hh == c
 
-    def set_off(n, e):
+    def set_off(n, e, arrays=(0, 1)):
         gathers = collector if n == 0 else jnp.logical_not(collector)
 
         @pl.when(gathers)
         def _():
-            for a in range(2):
+            for a in arrays:
                 s1_arrived(a, e)
                 ring(a, n, e).start()
                 if (n, e) == (0, 0):
@@ -221,7 +232,7 @@
 
         @pl.when(jnp.logical_not(gathers))
         def _():
-            for a in range(2):
+            for a in arrays:
                 if (n, e) == (0, 0):
 
                     @pl.when(away)
@@ -301,6 +312,8 @@
 
     set_off(0, 1)
     s1_sends(True)
+    s1_sends(False, (2,))
+    s1_sends(True, (2,))
     set_off(1, 0)
 
     for j in range(1, 8):
@@ -400,21 +413,46 @@
                     for e in range(2):
                         ring(a, 6, e).start()
 
-    ring_step(0)
-    for k in range(4):
-        ring_step(k + 1)
-
+    def relay_away(k):
         @pl.when(away)
         def _():
             relay(k)
 
+    def rest_step(n):
+        for e in range(2):
+            ring(2, n, e).wait_recv()
+            if n < 4:
+                ring(2, n + 2, e).start()
+            across(2, n + 1, e).start()
+        if n >= 4 and n < 6:
+
+            @pl.when(collector if n == 4 else jnp.logical_not(collector))
+            def _():
+                for e in range(2):
+                    ring(2, 6, e).start()
+
+    ring_step(0)
+    ring_step(1)
+    ring_step(2)
+    relay_away(0)
+    ring_step(3)
+    relay_away(1)
+    ring_step(4)
+    relay_away(2)
+    ring_step(5)
+    for n in range(2):
+        for e in range(2):
+            set_off(n, e, (2,))
+    relay_away(3)
+
     def project(a, zo, first, part=None):
-        acc, big = ((kacc, bigk), (qacc, bigq))[a]
+        acc, big = (kacc, qacc, qacc)[a], gathered[a]
+        lanes = (slice(None), lanes_a, lanes_b)[a]
         cols = pl.ds(pl.multiple_of(zo * 640, 128), 640)
 
         at = slice(None) if part is None else pl.ds(pl.multiple_of(part * 256, 256), 256)
         term = jnp.dot(rows[at, cols], big[zo], preferred_element_type=F32)
-        acc[at, :] = term if first else acc[at, :] + term
+        acc[at, lanes] = term if first else acc[at, lanes] + term
 
     def at_distance(d):
         return lax.rem(z + d + 8, 8)
@@ -435,15 +473,24 @@
                 for e in range(2):
                     across(a, n, e).wait_recv()
 
+    def last_in(a, e):
+        ring(a, 6, e).wait_recv()
+        across(a, 7, e).start()
+
     crossed(1, 2, 3, 4)
     near_slices(yl)
-    ring_step(5)
+    for a in range(2):
+        for e in range(2):
+            last_in(a, e)
+    rest_step(0)
     for k in range(4):
         for p in range(2):
             r2(p, k, 1 - yl).wait_recv()
 
     shares(True, True)
+    rest_step(1)
     near_slices(1 - yl)
+    rest_step(2)
     crossed(5, 6)
 
     @pl.loop(0, 2)
@@ -452,17 +499,11 @@
             project(a, at_distance(3 - 6 * i), False)
 
 
-    def last_in(a, e):
-        ring(a, 6, e).wait_recv()
-        across(a, 7, e).start()
-
     def last_step(a):
         for e in range(2):
             across(a, 7, e).wait_recv()
         project(a, at_distance(4), False)
 
-    last_in(0, 0)
-    last_in(0, 1)
 
     def turned(pre, at):
         inverse = lax.rsqrt(jnp.mean(pre * pre, axis=1, keepdims=True) + 1e-06)
@@ -470,6 +511,7 @@
         rotated = normed * cosb[at, :] + pltpu.roll(normed, HEAD_SIZE // 2, 1) * sinb[at, :]
         return inverse, normed, rotated.astype(BF)
 
+    rest_step(3)
     last_step(0)
 
     @pl.loop(0, 4)
@@ -484,9 +526,8 @@
         return remote(spot, spot, s_k, r_k, mate)
 
     keys(m).start()
-    last_in(1, 0)
-    last_in(1, 1)
     last_step(1)
+    rest_step(4)
 
     for hd in range(4):
         own = home & (hd == 2 * yl + c)
@@ -693,11 +734,23 @@
         1, (1 - m) * KW, (own_b, sib_b, got_b, arr_b, out_b, last_b, lgot_b, larr_b, fin_b)
     )
 
-    attend(2 * m, 3)
+    attend(2 * m, 1)
+    rest_step(5)
+    attend(2 * m + 1, 2)
     part_a.start()
+    rest_step(6)
+    for n in range(1, 8):
+        for e in range(2):
+            across(2, n, e).wait_recv()
+    project(2, 0, True)
+
+    @pl.loop(1, 8)
+    def _(i):
+        project(2, i, False)
+
+    part_a.middle(2)
     keys(1 - m).wait_recv()
     attend(3 - 3 * m, 2)
-    part_a.middle(2)
     part_b.start()
     part_a.middle(3)
     part_b.middle(2)
@@ -725,7 +778,7 @@
 
         @pl.when(jnp.logical_not(own))
         def _():
-            for a in range(2):
+            for a in range(3):
                 s1(a, t).wait_send()
 
         own_r = (2 * pair + t == x) & home
@@ -743,7 +796,7 @@
                 share(0, t, y2).wait_send()
                 share(1, t, y2).wait_send()
 
-    for a in range(2):
+    for a in range(3):
         for e in range(2):
             for n in range(7):
                 ring(a, n, e).wait_send()
@@ -792,16 +845,16 @@
         in_specs=[pl.BlockSpec(memory_space=pltpu.SMEM)] + [hbm] * 7,
         out_specs=(vmem,) * 4,
         scratch_shapes=[
-            v((SLICE, 640)), v((128, 5120)), v((SLICE, KW)), v((8, 640, 640)), v((8, 640, KW)),
+            v((SLICE, 640)), v((128, 5120)), v((SLICE, KW)), v((8, 640, KW)), v((8, 640, 256)), v((8, 640, KW)),
             v((512, 5120)), v((512, 640)), v((512, 640)), v((128, 5120)),
             v((2, SLICE, 256)), v((3, 512), jnp.int32), v((32, 128), F32), v((2, 640, 256)), v((4, 2, 8, 640), F32), v((4, 2, 8, 256), F32),
             v((8, 2, 640), F32), v((8, 2, 640), F32), v((2, 5120), F32),
             v((3, 512), jnp.int32), v((8, 512), F32), v((512, 128), F32), v((512, 128), F32),
             v((512, 640), F32), v((512, KW), F32), v((512, 640)), v((512, 640)),
             *sums_of(KW), *sums_of(256),
-            dma((7,)), dma((2,)), dma, dma,
-            dma((4,)), dma((4,)), dma((8,)), dma((8,)), dma((2, 2)), dma((2, 2)),
-            dma((2, 7, 2)), dma((2, 7, 2)), dma((2, 8, 2)), dma((2, 8, 2)),
+            dma((8,)), dma((2,)), dma, dma,
+            dma((4,)), dma((4,)), dma((8,)), dma((8,)), dma((3, 2)), dma((3, 2)),
+            dma((3, 7, 2)), dma((3, 7, 2)), dma((3, 8, 2)), dma((3, 8, 2)),
             dma((2, 4)), dma((2, 4)), dma((2, 4)), dma((2, 4)), dma((2, 2, 2)), dma((2, 4)),
             dma, dma,
             dma((2, 7)), dma((2, 7)), dma((2, 7, 2)), dma((2, 7, 2)), dma((2, 2)), dma((2, 2)),

time: 124 us -> 124 us (level); the launches traced: 124 us -> 122 us
    pallas_call x1, Pallas kernels: 122 us -> 121 us  [step(): pl.pallas_call(kernel, out_shape=(jax.ShapeDtypeStruct((2, SLICE, 640), B...]
where the time goes in v6:
time: 124 us; the launch traced here: 122 us
  Pallas kernels  121 us (98%)
    pallas_call x1, Pallas kernels, step(): pl.pallas_call(kernel, out_shape=(jax.ShapeDtypeStruct((2, SLICE, 640), B...  121 us

profile of v6, /device:TPU:1, one launch (start us, length us, event | category | flops | bytes accessed | tf_op | source)
XLA Modules:
  0.0 122.5 jit_solution(13774239975834415506)
XLA Ops:
  0.6 120.7 %fisher_step.1 = (bf16[2,160,640]{2,1,0:T(8,128)(2,1)S(1)}, bf16[160,640]{1,0:T(8,128)(2,1)S(1)}, bf16[160,640]{1,0:T(8,128)(2,1)S(1)}, bf16[160,640]{1,0:T(8,128)(2,1)S(1)}) custom-call(s32[32]{0:T(128)} %when.1, bf16[2,160,256]{2,1,0:T(8,128)(2,1)} %bitcast.12, s32[3,512]{1,0:T(4,128)} %lat_hbm.1, bf16[128,5120]{1,0:T(8,128)(2,1)} %tok_hbm.1, ...), custom_call_target="tpu_custom_call" | custom-call | tf_op jit(solution)/shard_map/fisher_step/pallas_call | solution.py:837
  121.3 1.1 add_divide_fusion

commit v7 on v6

--- a/solution.py
+++ b/solution.py
@@ -467,6 +467,12 @@
             for a in range(2):
                 project(a, at_distance(d), False, part)
 
+    def far_slices(part):
+        @pl.loop(0, 2)
+        def _(i):
+            for a in range(2):
+                project(a, at_distance(3 - 6 * i), False, part)
+
     def crossed(*steps):
         for n in steps:
             for a in range(2):
@@ -483,26 +489,24 @@
         for e in range(2):
             last_in(a, e)
     rest_step(0)
+    shares(True, True)
+    crossed(5, 6)
+    far_slices(yl)
+    crossed(7)
+    for a in range(2):
+        project(a, at_distance(4), False, yl)
     for k in range(4):
         for p in range(2):
             r2(p, k, 1 - yl).wait_recv()
 
-    shares(True, True)
     rest_step(1)
     near_slices(1 - yl)
     rest_step(2)
-    crossed(5, 6)
-
-    @pl.loop(0, 2)
-    def _(i):
-        for a in range(2):
-            project(a, at_distance(3 - 6 * i), False)
-
+
+    far_slices(1 - yl)
 
     def last_step(a):
-        for e in range(2):
-            across(a, 7, e).wait_recv()
-        project(a, at_distance(4), False)
+        project(a, at_distance(4), False, 1 - yl)
 
 
     def turned(pre, at):

time: 124 us -> 128 us (1.032)
  Pallas kernels: 121 us -> 126 us
    pallas_call x1, Pallas kernels: 121 us -> 126 us  [step(): pl.pallas_call(kernel, out_shape=(jax.ShapeDtypeStruct((2, SLICE, 640), B...]
where the time goes in v7:
time: 128 us
  Pallas kernels  126 us (98%)
    pallas_call x1, Pallas kernels, step(): pl.pallas_call(kernel, out_shape=(jax.ShapeDtypeStruct((2, SLICE, 640), B...  126 us

profile of v7, /device:TPU:1, one launch (start us, length us, event | category | flops | bytes accessed | tf_op | source)
XLA Modules:
  0.0 127.7 jit_solution(5466798317003233553)
XLA Ops:
  0.6 125.9 %fisher_step.1 = (bf16[2,160,640]{2,1,0:T(8,128)(2,1)S(1)}, bf16[160,640]{1,0:T(8,128)(2,1)S(1)}, bf16[160,640]{1,0:T(8,128)(2,1)S(1)}, bf16[160,640]{1,0:T(8,128)(2,1)S(1)}) custom-call(s32[32]{0:T(128)} %when.1, bf16[2,160,256]{2,1,0:T(8,128)(2,1)} %bitcast.12, s32[3,512]{1,0:T(4,128)} %lat_hbm.1, bf16[128,5120]{1,0:T(8,128)(2,1)} %tok_hbm.1, ...), custom_call_target="tpu_custom_call" | custom-call | tf_op jit(solution)/shard_map/fisher_step/pallas_call | solution.py:841
  126.5 1.1 add_divide_fusion
